TPU v7x, 32 devices: a whole 2x2x4 slice. The times are simulated.
32 devices in a mesh: grp: 16 (over z, x, core), mode: 2 (over y).
Axes of the slice: x: 2, y: 2, z: 4, core: 2. Of those that a mesh axis runs over, the one named last changes fastest.
Arguments:
- probe: float32 [2, 8, 512, 512], P(None, 'mode'), may hold values from -3 to 3
- prev_direction: float32 [2, 8, 512, 512], P(None, 'mode'), may hold values from -0.6 to 0.6
- prev_norm: float32 [8], P('mode'), may hold values from 0.5 to 4
- object_tile: bfloat16 [2, 10240, 640], P(None, 'grp'), may hold values from -4 to 4
- offsets: int32 [32, 2], P('grp'), may hold values from 0 to 128
- amplitude: bfloat16 [32, 512, 512], P('grp'), may hold values from 0.5 to 3.5
Outputs:
- new_probe: float32 [2, 8, 512, 512], P(None, 'mode')
- new_direction: float32 [2, 8, 512, 512], P(None, 'mode')
- new_norm: float32 [8], P('mode')
All inputs are finite; a program needn't handle non-finite values.
Results may differ from a plain program's by a relative error of at most 0.0045.
Values sent between devices are 32-bit elements; how exact they have to be, the bound alone decides.
A program may use at most 128 MiB of HBM per device.

v0:
```python
import functools
import math

import jax
import jax.numpy as jnp
from jax import lax
from jax.experimental import pallas as pl
from jax.experimental.pallas import tpu as pltpu
from jax.sharding import PartitionSpec as P

VMEM_LIMIT = 60 * 1024 * 1024
TILE = 256


def base_table(width):
    index = jnp.arange(width, dtype=jnp.int32)
    product = index[:, None] * index[None, :] % width
    angle = -2.0 * math.pi / width * product.astype(jnp.float32)
    scale = 1.0 / math.sqrt(width)
    real_part = (jnp.cos(angle) * scale).astype(jnp.bfloat16)
    imag_part = (jnp.sin(angle) * scale).astype(jnp.bfloat16)
    return jnp.stack([real_part, imag_part])


def build_pair(base_ref, plus, minus):
    width = base_ref.shape[1]
    cosine, sine = base_ref[0], base_ref[1]
    for ref, sign in ((plus, 1), (minus, -1)):
        ref[:width, :width] = cosine
        ref[width:, width:] = cosine
        ref[:width, width:] = sine if sign > 0 else -sine
        ref[width:, :width] = -sine if sign > 0 else sine


def transform(joined, stacked, right, left, emit):
    width = joined.shape[0]
    tile = min(TILE, width)

    def first(step, carry):
        at = pl.multiple_of(step * tile, tile)
        half = jnp.dot(joined[pl.ds(at, tile), :], right[...], preferred_element_type=jnp.float32)
        half = half.astype(jnp.bfloat16)
        stacked[pl.ds(at, tile), :] = half[:, :width]
        stacked[pl.ds(at + width, tile), :] = half[:, width:]
        return carry

    def second(step, carry):
        at = pl.multiple_of(step * tile, tile)
        rows = pl.ds(at, tile)
        real = jnp.dot(left[rows, :], stacked[...], preferred_element_type=jnp.float32)
        imag = jnp.dot(left[pl.ds(at + width, tile), :], stacked[...], preferred_element_type=jnp.float32)
        emit(rows, real, imag)
        return carry

    lax.fori_loop(0, width // tile, first, 0)
    lax.fori_loop(0, width // tile, second, 0)


def forward_kernel(base_ref, probe_ref, patch_ref, wave_ref, exit_ref, sum_ref, plus, minus, joined, stacked):
    mode = pl.program_id(0)
    width = sum_ref.shape[0]
    tile = 64

    @pl.when(mode == 0)
    def _():
        build_pair(base_ref, plus, minus)
        sum_ref[...] = jnp.zeros_like(sum_ref)

    def leave(step, carry):
        rows = pl.ds(pl.multiple_of(step * tile, tile), tile)
        obj_re = patch_ref[0, rows, :].astype(jnp.float32)
        obj_im = patch_ref[1, rows, :].astype(jnp.float32)
        pro_re, pro_im = probe_ref[0, 0, rows, :], probe_ref[1, 0, rows, :]
        exit_re = (pro_re * obj_re - pro_im * obj_im).astype(jnp.bfloat16)
        exit_im = (pro_re * obj_im + pro_im * obj_re).astype(jnp.bfloat16)
        joined[rows, :width] = exit_re
        joined[rows, width:] = exit_im
        exit_ref[0, 0, rows, :] = exit_re
        exit_ref[0, 1, rows, :] = exit_im
        return carry

    lax.fori_loop(0, width // tile, leave, 0)

    def emit(rows, real, imag):
        wave_ref[0, 0, rows, :] = real
        wave_ref[0, 1, rows, :] = imag
        sum_ref[rows, :] += real * real + imag * imag

    transform(joined, stacked, plus, minus, emit)


def backward_kernel(first, base_ref, total_ref, amp_ref, wave_ref, exit_ref, patch_ref, *rest):
    if first:
        grad_in, (grad_ref, plus, minus, joined, stacked, ratio) = None, rest
    else:
        grad_in, grad_ref, plus, minus, joined, stacked, ratio = rest
    width = total_ref.shape[0]
    tile = 64

    @pl.when(pl.program_id(0) == 0)
    def _():
        build_pair(base_ref, plus, minus)

        def scale(step, carry):
            rows = pl.ds(pl.multiple_of(step * tile, tile), tile)
            ratio[rows, :] = amp_ref[0, rows, :].astype(jnp.float32) / jnp.sqrt(total_ref[rows, :] + 1.0)
            return carry

        lax.fori_loop(0, width // tile, scale, 0)

    def fix(step, carry):
        rows = pl.ds(pl.multiple_of(step * tile, tile), tile)
        joined[rows, :width] = (ratio[rows, :] * wave_ref[0, 0, rows, :]).astype(jnp.bfloat16)
        joined[rows, width:] = (ratio[rows, :] * wave_ref[0, 1, rows, :]).astype(jnp.bfloat16)
        return carry

    lax.fori_loop(0, width // tile, fix, 0)

    def emit(rows, real, imag):
        obj_re = patch_ref[0, rows, :].astype(jnp.float32)
        obj_im = patch_ref[1, rows, :].astype(jnp.float32)
        diff_re = real - exit_ref[0, 0, rows, :].astype(jnp.float32)
        diff_im = imag - exit_ref[0, 1, rows, :].astype(jnp.float32)
        add_re = obj_re * diff_re + obj_im * diff_im
        add_im = obj_re * diff_im - obj_im * diff_re
        if grad_in is not None:
            add_re = grad_in[0, 0, rows, :] + add_re
            add_im = grad_in[0, 1, rows, :] + add_im
        grad_ref[0, 0, rows, :] = add_re
        grad_ref[0, 1, rows, :] = add_im

    transform(joined, stacked, minus, plus, emit)


def finish_kernel(norm_ref, grad_ref, illum_ref, probe_ref, dir_ref, new_probe, new_dir, new_norm):
    mode = pl.program_id(0)
    width = illum_ref.shape[0]
    tile = 32
    steps = width // tile
    pixels = float(width * width)

    def rows_of(step):
        return pl.ds(pl.multiple_of(step * tile, tile), tile)

    def fold(block):
        return jnp.sum(block.reshape(tile // 8, 8, width), axis=0)

    zero = jnp.zeros((8, width), jnp.float32)
    total = jnp.sum(lax.fori_loop(0, steps, lambda i, acc: acc + fold(illum_ref[rows_of(i), :]), zero))
    shift = total / pixels

    def one(step, acc):
        rows = rows_of(step)
        den = illum_ref[rows, :] + shift
        g_re, g_im = grad_ref[0, 0, rows, :], grad_ref[0, 1, rows, :]
        p_re, p_im = g_re / den, g_im / den
        new_dir[0, 0, rows, :] = p_re
        new_dir[1, 0, rows, :] = p_im
        return acc + fold(g_re * p_re + g_im * p_im)

    norm = jnp.sum(lax.fori_loop(0, steps, one, zero)) / pixels
    new_norm[mode] = norm
    beta = norm / norm_ref[mode]

    def two(step, acc):
        rows = rows_of(step)
        upper, lower = acc
        d_re = new_dir[0, 0, rows, :] + beta * dir_ref[0, 0, rows, :]
        d_im = new_dir[1, 0, rows, :] + beta * dir_ref[1, 0, rows, :]
        new_dir[0, 0, rows, :] = d_re
        new_dir[1, 0, rows, :] = d_im
        upper = upper + fold(grad_ref[0, 0, rows, :] * d_re + grad_ref[0, 1, rows, :] * d_im)
        lower = lower + fold(illum_ref[rows, :] * (d_re * d_re + d_im * d_im))
        return (upper, lower)

    upper, lower = lax.fori_loop(0, steps, two, (zero, zero))
    alpha = (jnp.sum(upper) / pixels) / (jnp.sum(lower) / pixels + 1.0)

    def three(step, carry):
        rows = rows_of(step)
        new_probe[0, 0, rows, :] = probe_ref[0, 0, rows, :] + alpha * new_dir[0, 0, rows, :]
        new_probe[1, 0, rows, :] = probe_ref[1, 0, rows, :] + alpha * new_dir[1, 0, rows, :]
        return carry

    lax.fori_loop(0, steps, three, 0)


def whole(shape):
    return pl.BlockSpec(shape, lambda *_: (0,) * len(shape))


def table_scratch(width):
    return [
        pltpu.VMEM((2 * width, 2 * width), jnp.bfloat16),
        pltpu.VMEM((2 * width, 2 * width), jnp.bfloat16),
        pltpu.VMEM((width, 2 * width), jnp.bfloat16),
        pltpu.VMEM((2 * width, width), jnp.bfloat16),
    ]


def params():
    return pltpu.CompilerParams(dimension_semantics=("arbitrary",), vmem_limit_bytes=VMEM_LIMIT)


def cost(modes, width, moved):
    return pl.CostEstimate(flops=modes * 16 * width**3, bytes_accessed=moved, transcendentals=0)


def forward(base, probe, patch):
    modes, width = probe.shape[1], probe.shape[2]
    return pl.pallas_call(
        forward_kernel,
        grid=(modes,),
        in_specs=[
            whole(base.shape),
            pl.BlockSpec((2, 1, width, width), lambda m: (0, m, 0, 0)),
            whole(patch.shape),
        ],
        out_specs=[
            pl.BlockSpec((1, 2, width, width), lambda m: (m, 0, 0, 0)),
            pl.BlockSpec((1, 2, width, width), lambda m: (m, 0, 0, 0)),
            whole((width, width)),
        ],
        out_shape=[
            jax.ShapeDtypeStruct((modes, 2, width, width), jnp.float32),
            jax.ShapeDtypeStruct((modes, 2, width, width), jnp.bfloat16),
            jax.ShapeDtypeStruct((width, width), jnp.float32),
        ],
        scratch_shapes=table_scratch(width),
        compiler_params=params(),
        cost_estimate=cost(modes, width, modes * width * width * 20),
        name="forward",
    )(base, probe, patch)


def backward(base, total, amplitude, index, wave, exits, patch, grad, start, count):
    width = total.shape[0]
    at = lambda m: (m + start, 0, 0, 0)
    block = (1, 2, width, width)
    operands = [base, total, amplitude, wave, exits, patch]
    in_specs = [
        whole(base.shape),
        whole(total.shape),
        pl.BlockSpec((1, width, width), lambda m: (index, 0, 0)),
        pl.BlockSpec(block, at),
        pl.BlockSpec(block, at),
        whole(patch.shape),
    ]
    if grad is not None:
        operands.append(grad)
        in_specs.append(pl.BlockSpec(block, at))
    return pl.pallas_call(
        functools.partial(backward_kernel, grad is None),
        grid=(count,),
        in_specs=in_specs,
        out_specs=pl.BlockSpec(block, lambda m: (m, 0, 0, 0)),
        out_shape=jax.ShapeDtypeStruct((count, 2, width, width), jnp.float32),
        scratch_shapes=table_scratch(width) + [pltpu.VMEM((width, width), jnp.float32)],
        compiler_params=params(),
        cost_estimate=cost(count, width, count * width * width * 24),
        name="backward",
    )(*operands)


def finish(prev_norm, grad, illum, probe, direction):
    modes, width = probe.shape[1], illum.shape[0]
    block = pl.BlockSpec((2, 1, width, width), lambda m: (0, m, 0, 0))
    return pl.pallas_call(
        finish_kernel,
        grid=(modes,),
        in_specs=[
            pl.BlockSpec(memory_space=pltpu.SMEM),
            pl.BlockSpec((1, 2, width, width), lambda m: (m, 0, 0, 0)),
            whole(illum.shape),
            block,
            block,
        ],
        out_specs=[block, block, pl.BlockSpec(memory_space=pltpu.SMEM)],
        out_shape=[
            jax.ShapeDtypeStruct(probe.shape, jnp.float32),
            jax.ShapeDtypeStruct(probe.shape, jnp.float32),
            jax.ShapeDtypeStruct((modes,), jnp.float32),
        ],
        compiler_params=params(),
        name="finish",
    )(prev_norm, grad, illum, probe, direction)


def sum_over_modes(local_sum):
    if lax.axis_size("mode") != 2:
        return lax.psum(local_sum, "mode")
    return local_sum + lax.ppermute(local_sum, "mode", [(0, 1), (1, 0)])


def on_device(probe, prev_direction, prev_norm, object_tile, offsets, amplitude):
    width = probe.shape[2]
    modes = probe.shape[1]
    positions = amplitude.shape[0]
    base = base_table(width)
    illum = jnp.zeros((width, width), jnp.float32)
    patches, kept = [], []
    for index in range(positions):
        patch = lax.dynamic_slice(
            object_tile, (jnp.int32(0), offsets[index, 0], offsets[index, 1]), (2, width, width)
        )
        patches.append(patch)
        wave, exits, local_sum = forward(base, probe, patch)
        total = sum_over_modes(local_sum)
        kept.append((wave, exits, total))
        wide = patch.astype(jnp.float32)
        illum = illum + wide[0] * wide[0] + wide[1] * wide[1]
    grad = None
    for index in range(positions - 1):
        wave, exits, total = kept[index]
        grad = backward(base, total, amplitude, index, wave, exits, patches[index], grad, 0, modes)
    wave, exits, total = kept[-1]
    part = backward(base, total, amplitude, positions - 1, wave, exits, patches[-1], grad, 0, modes)
    part, illum = lax.psum((part, illum), "grp")
    return tuple(finish(prev_norm, part, illum, probe, prev_direction))


def solution(mesh):
    return jax.shard_map(
        on_device,
        mesh=mesh,
        in_specs=(
            P(None, "mode", None, None),
            P(None, "mode", None, None),
            P("mode"),
            P(None, "grp", None),
            P("grp", None),
            P("grp", None, None),
        ),
        out_specs=(P(None, "mode", None, None), P(None, "mode", None, None), P("mode")),
        check_vma=False,
    )
```

profile of v0, /device:TPU:0, one launch (start us, length us, event | category | flops | bytes accessed | tf_op | source)
XLA Modules:
  0.0 322.2 jit_solution(16310647379972051351)
XLA Ops:
  7.2 0.0 copy-start
  7.2 0.0 all-reduce.3.cloned.1.call-start
  7.2 1.4 fusion.12
  13.8 4.4 %multiply_convert_fusion = (bf16[1,512,512]{2,1,0:T(8,128)(2,1)S(1)}, bf16[1,512,512]{2,1,0:T(8,128)(2,1)S(1)}) fusion(), kind=kLoop, calls=%fused_computation.15 | loop fusion | flops 4718592 | bytes 1048576 | tf_op jit(solution)/shard_map/convert_element_type | solution.py:21
  20.8 1.1 pad_maximum_fusion.base_ref
  21.9 0.0 copy-done
  21.9 3.2 fusion.10
  25.0 17.9 %forward.3 = (f32[4,2,512,512]{3,2,1,0:T(8,128)}, bf16[4,2,512,512]{3,2,1,0:T(8,128)(2,1)}, f32[512,512]{1,0:T(8,128)}) custom-call(bf16[2,512,512]{2,1,0:T(8,128)(2,1)} %pad_maximum_fusion.base_ref, f32[2,4,512,512]{3,2,1,0:T(8,128)} %probe_ref.5, bf16[2,512,512]{2,1,0:T(8,128)(2,1)} %get-tuple-element.18.patch_ref), custom_call_target="tpu_custom_call" | custom-call | flops 8589934592 | bytes 20971520 | tf_op jit(solution)/shard_map/forward/pallas_call | solution.py:211
  42.9 3.1 collective-permute-start.1
  46.0 17.9 %forward.2 = (f32[4,2,512,512]{3,2,1,0:T(8,128)}, bf16[4,2,512,512]{3,2,1,0:T(8,128)(2,1)}, f32[512,512]{1,0:T(8,128)}) custom-call(bf16[2,512,512]{2,1,0:T(8,128)(2,1)} %pad_maximum_fusion.base_ref, f32[2,4,512,512]{3,2,1,0:T(8,128)} %probe_ref.5, bf16[2,512,512]{2,1,0:T(8,128)(2,1)} %get-tuple-element.22.patch_ref), custom_call_target="tpu_custom_call" | custom-call | flops 8589934592 | bytes 20971520 | tf_op jit(solution)/shard_map/forward/pallas_call | solution.py:211
  63.9 0.0 copy-start.2
  63.9 0.1 collective-permute-start
  64.0 3.1 fusion.4
  67.1 3.2 collective-permute-done.1
  70.3 0.0 copy-done.2
  70.3 2.4 add.61.total_ref
  72.7 0.0 copy-start.1
  72.7 18.3 %backward.2.rest_0_ = f32[4,2,512,512]{3,2,1,0:T(8,128)} custom-call(bf16[2,512,512]{2,1,0:T(8,128)(2,1)} %pad_maximum_fusion.base_ref, f32[512,512]{1,0:T(8,128)} %add.61.total_ref, bf16[2,512,512]{2,1,0:T(8,128)(2,1)} %amp_ref.3, f32[4,2,512,512]{3,2,1,0:T(8,128)} %get-tuple-element.13.wave_ref, bf16[4,2,512,512]{3,2,1,0:T(8,128)(2,1)} %get-tuple-element.14.exit_ref, ...), custom_call_target="tpu_custom_call" | custom-call | flops 8589934592 | bytes 25165824 | tf_op jit(solution)/shard_map/backward/pallas_call | solution.py:252
  91.1 0.8 collective-permute-done
  91.8 0.0 copy-done.1
  91.8 1.3 add.58.total_ref
  93.1 19.5 %backward.3 = f32[4,2,512,512]{3,2,1,0:T(8,128)} custom-call(bf16[2,512,512]{2,1,0:T(8,128)(2,1)} %pad_maximum_fusion.base_ref, f32[512,512]{1,0:T(8,128)} %add.58.total_ref, bf16[2,512,512]{2,1,0:T(8,128)(2,1)} %amp_ref.3, f32[4,2,512,512]{3,2,1,0:T(8,128)} %get-tuple-element.10.wave_ref, bf16[4,2,512,512]{3,2,1,0:T(8,128)(2,1)} %get-tuple-element.11.exit_ref, ...), custom_call_target="tpu_custom_call" | custom-call | flops 8589934592 | bytes 25165824 | tf_op jit(solution)/shard_map/backward/pallas_call | solution.py:252
  112.6 0.0 all-reduce.3.cloned.1.call-update
  112.6 186.3 %all-reduce.3.cloned.1.call-done = (f32[4,2,512,512]{3,2,1,0:T(8,128)}, f32[512,512]{1,0:T(8,128)}) async-done(((f32[4,2,512,512]{3,2,1,0:T(8,128)}, f32[512,512]{1,0:T(8,128)}), (f32[4,2,512,512]{3,2,1,0:T(8,128)}, f32[512,512]{1,0:T(8,128)})) %all-reduce.3.cloned.1.call-update) | async-done | bytes 9437200 | tf_op jit(solution)/shard_map/psum | solution.py:318
  298.9 16.5 %finish.1 = (f32[2,4,512,512]{3,2,1,0:T(8,128)}, f32[2,4,512,512]{3,2,1,0:T(8,128)}, f32[4]{0:T(128)}) custom-call(f32[4]{0:T(128)} %norm_ref.1, f32[4,2,512,512]{3,2,1,0:T(8,128)} %get-tuple-element.15.grad_ref, f32[512,512]{1,0:T(8,128)} %get-tuple-element.16.illum_ref, f32[2,4,512,512]{3,2,1,0:T(8,128)} %probe_ref.5, f32[2,4,512,512]{3,2,1,0:T(8,128)} %dir_ref.1), custom_call_target="tpu_custom_call" | custom-call | tf_op jit(solution)/shard_map/finish/pallas_call | solution.py:268
Async XLA Ops:
  7.2 14.7 %copy-start = (bf16[2,640,640]{2,1,0:T(8,128)(2,1)S(1)}, bf16[2,640,640]{2,1,0:T(8,128)(2,1)}, u32[]{:S(2)}) copy-start(bf16[2,640,640]{2,1,0:T(8,128)(2,1)} %param.9) | copy-start | bytes 4915204
  7.2 291.7 %all-reduce.3.cloned.1.call-start = ((), (), s32[]{:S(2)}) async-start(), calls=%async_computation | async-start | bytes 18874368 | tf_op jit(solution)/shard_map/psum | solution.py:318
  42.9 27.4 %collective-permute-start.1 = (f32[512,512]{1,0:T(8,128)}, f32[512,512]{1,0:T(8,128)}, u32[]{:S(2)}, u32[]{:S(2)}) collective-permute-start(f32[512,512]{1,0:T(8,128)} %get-tuple-element.12), channel_id=1, source_target_pairs={{0,1},{1,0},{2,3},{3,2},{4,5},{5,4},{6,7},{7,6},{8,9},{9,8},{10,11... | collective-permute-start | bytes 3145736 | tf_op jit(solution)/shard_map/ppermute | solution.py:292
  63.9 6.4 %copy-start.2 = (f32[512,512]{1,0:T(8,128)S(1)}, f32[512,512]{1,0:T(8,128)}, u32[]{:S(2)}) copy-start(f32[512,512]{1,0:T(8,128)} %get-tuple-element.12) | copy-start | bytes 3145732
  63.9 27.9 %collective-permute-start = (f32[512,512]{1,0:T(8,128)}, f32[512,512]{1,0:T(8,128)S(1)}, u32[]{:S(2)}, u32[]{:S(2)}) collective-permute-start(f32[512,512]{1,0:T(8,128)} %get-tuple-element.9), channel_id=1, source_target_pairs={{0,1},{1,0},{2,3},{3,2},{4,5},{5,4},{6,7},{7,6},{8,9},{9,8},{10,11... | collective-permute-start | bytes 3145736 | tf_op jit(solution)/shard_map/ppermute | solution.py:292
  72.7 19.1 %copy-start.1 = (f32[512,512]{1,0:T(8,128)S(1)}, f32[512,512]{1,0:T(8,128)}, u32[]{:S(2)}) copy-start(f32[512,512]{1,0:T(8,128)} %get-tuple-element.9) | copy-start | bytes 3145732
Sparse Core Ops, SparseCore 0:
  112.7 186.1 all-reduce.2
where the time goes:
time: 322 us
  waiting for transfers between devices  190 us (59%)
  Pallas kernels  90.1 us (28%)
  between operations  21.8 us (7%)
  other arithmetic  15.4 us (5%)
    psum x1, waiting for transfers between devices, on_device(): part, illum = lax.psum((part, illum), 'grp')  186 us
    pallas_call x2, Pallas kernels, backward(): pl.pallas_call(functools.partial(backward_kernel, grad is None), grid=(co...  37.8 us
    pallas_call x2, Pallas kernels, forward(): pl.pallas_call(forward_kernel, grid=(modes,), in_specs=[whole(base.shape)...  35.8 us
    pallas_call x1, Pallas kernels, finish(): pl.pallas_call(finish_kernel, grid=(modes,), in_specs=[pl.BlockSpec(memor...  16.5 us
  transfers between devices with their start and end apart: 3, of which 3 were waited for; matrix products, arithmetic and copies ran while one was open for 2% of the time, Pallas kernels for 11%

commit v1 on v0

--- a/solution.py
+++ b/solution.py
@@ -8,6 +8,7 @@
 from jax.experimental.pallas import tpu as pltpu
 from jax.sharding import PartitionSpec as P
 
+MESH = pl.DeviceIdType.MESH
 VMEM_LIMIT = 60 * 1024 * 1024
 TILE = 256
 
@@ -132,57 +133,130 @@
     transform(joined, stacked, minus, plus, emit)
 
 
-def finish_kernel(norm_ref, grad_ref, illum_ref, probe_ref, dir_ref, new_probe, new_dir, new_norm):
-    mode = pl.program_id(0)
-    width = illum_ref.shape[0]
-    tile = 32
-    steps = width // tile
-    pixels = float(width * width)
-
-    def rows_of(step):
-        return pl.ds(pl.multiple_of(step * tile, tile), tile)
-
-    def fold(block):
-        return jnp.sum(block.reshape(tile // 8, 8, width), axis=0)
-
-    zero = jnp.zeros((8, width), jnp.float32)
-    total = jnp.sum(lax.fori_loop(0, steps, lambda i, acc: acc + fold(illum_ref[rows_of(i), :]), zero))
-    shift = total / pixels
-
-    def one(step, acc):
-        rows = rows_of(step)
-        den = illum_ref[rows, :] + shift
-        g_re, g_im = grad_ref[0, 0, rows, :], grad_ref[0, 1, rows, :]
-        p_re, p_im = g_re / den, g_im / den
-        new_dir[0, 0, rows, :] = p_re
-        new_dir[1, 0, rows, :] = p_im
-        return acc + fold(g_re * p_re + g_im * p_im)
-
-    norm = jnp.sum(lax.fori_loop(0, steps, one, zero)) / pixels
-    new_norm[mode] = norm
-    beta = norm / norm_ref[mode]
-
-    def two(step, acc):
-        rows = rows_of(step)
-        upper, lower = acc
-        d_re = new_dir[0, 0, rows, :] + beta * dir_ref[0, 0, rows, :]
-        d_im = new_dir[1, 0, rows, :] + beta * dir_ref[1, 0, rows, :]
-        new_dir[0, 0, rows, :] = d_re
-        new_dir[1, 0, rows, :] = d_im
-        upper = upper + fold(grad_ref[0, 0, rows, :] * d_re + grad_ref[0, 1, rows, :] * d_im)
-        lower = lower + fold(illum_ref[rows, :] * (d_re * d_re + d_im * d_im))
-        return (upper, lower)
-
-    upper, lower = lax.fori_loop(0, steps, two, (zero, zero))
-    alpha = (jnp.sum(upper) / pixels) / (jnp.sum(lower) / pixels + 1.0)
-
-    def three(step, carry):
-        rows = rows_of(step)
-        new_probe[0, 0, rows, :] = probe_ref[0, 0, rows, :] + alpha * new_dir[0, 0, rows, :]
-        new_probe[1, 0, rows, :] = probe_ref[1, 0, rows, :] + alpha * new_dir[1, 0, rows, :]
-        return carry
-
-    lax.fori_loop(0, steps, three, 0)
+def fold_lanes(block):
+    rows, width = block.shape
+    lanes = min(128, width)
+    acc = jnp.sum(block.reshape(rows // 8, 8, width), axis=0)
+    out = acc[:, :lanes]
+    for at in range(lanes, width, lanes):
+        out = out + acc[:, at : at + lanes]
+    return out
+
+
+class Spot:
+    def __init__(self, outer, inner, cores):
+        me = lax.axis_index("grp")
+        self.me = me
+        self.sizes = (outer, inner, cores)
+        self.count = outer * inner * cores
+        self.core = lax.rem(me, cores)
+        self.inner = lax.rem(me // cores, inner)
+        self.outer = me // (cores * inner)
+        self.stride = {"core": 1, "inner": cores, "outer": cores * inner}
+
+    def at(self, line, step):
+        return {"grp": self.me + step * self.stride[line]}
+
+    def partner(self):
+        return {"grp": self.me + 1 - 2 * self.core}
+
+
+def remote(src, dst, send, recv, device):
+    return pltpu.make_async_remote_copy(
+        src_ref=src, dst_ref=dst, send_sem=send, recv_sem=recv, device_id=device, device_id_type=MESH
+    )
+
+
+class Line:
+    def __init__(self, spot, name, length, place):
+        self.spot, self.name, self.length, self.place = spot, name, length, place
+
+    def scatter(self, chunk, slots, send, recv):
+        size, u = self.length, self.place
+
+        def take(slot, into):
+            got = remote(slots.at[slot], slots.at[slot], send.at[0], recv.at[slot], self.spot.at(self.name, 0))
+            got.wait_recv()
+            into[...] += slots[slot]
+
+        def push(k, step, slot):
+            remote(chunk(k), slots.at[slot], send.at[k], recv.at[slot], self.spot.at(self.name, step)).start()
+
+        for step in range(size - 1):
+            right, left = size - 1 - step, step
+
+            @pl.when(u < right)
+            def _():
+                @pl.when(u > 0)
+                def _():
+                    take(right + 1, chunk(right))
+
+                push(right, 1, right + 1)
+
+            @pl.when(u > left)
+            def _():
+                @pl.when(u < size - 1)
+                def _():
+                    take(left, chunk(left))
+
+                push(left, -1, left)
+
+            yield
+
+        @pl.when(u > 0)
+        def _():
+            take(u + 1, chunk(u))
+
+        @pl.when(u < size - 1)
+        def _():
+            take(u, chunk(u))
+
+    def scatter_end(self, chunk, slots, send, recv):
+        for k in range(self.length):
+            @pl.when(self.place != k)
+            def _():
+                remote(chunk(k), slots.at[0], send.at[k], recv.at[0], self.spot.at(self.name, 0)).wait_send()
+
+    def gather(self, chunk, send, recv):
+        size, u = self.length, self.place
+
+        def push(k, way, step):
+            remote(chunk(k), chunk(k), send.at[way, k], recv.at[k], self.spot.at(self.name, step)).start()
+
+        def take(k):
+            remote(chunk(k), chunk(k), send.at[0, 0], recv.at[k], self.spot.at(self.name, 0)).wait_recv()
+
+        for step in range(size):
+            low, high = u - step, u + step
+
+            @pl.when(low >= 0)
+            def _():
+                if step > 0:
+                    take(low)
+
+                @pl.when(u < size - 1)
+                def _():
+                    push(low, 0, 1)
+
+            @pl.when(high < size)
+            def _():
+                if step > 0:
+                    take(high)
+
+                @pl.when(u > 0)
+                def _():
+                    push(high, 1, -1)
+
+            if step < size - 1:
+                yield
+
+    def gather_end(self, chunk, send, recv):
+        size, u = self.length, self.place
+        for k in range(size):
+            for way in range(2):
+                @pl.when((u < size - 1) & (u >= k) if way == 0 else (u > 0) & (u <= k))
+                def _():
+                    remote(chunk(k), chunk(k), send.at[way, k], recv.at[k], self.spot.at(self.name, 0)).wait_send()
 
 
 def whole(shape):
@@ -262,28 +336,324 @@
     )(*operands)
 
 
-def finish(prev_norm, grad, illum, probe, direction):
-    modes, width = probe.shape[1], illum.shape[0]
-    block = pl.BlockSpec((2, 1, width, width), lambda m: (0, m, 0, 0))
+def split_lines(cores_total):
+    cores = 2 if cores_total % 2 == 0 else 1
+    chips = cores_total // cores
+    inner = 1
+    while inner * inner * 2 <= chips and chips % (inner * 2) == 0:
+        inner *= 2
+    inner = inner if inner * inner <= chips else inner // 2
+    return chips // inner, inner, cores
+
+
+class Shares:
+    def __init__(self, spot, width):
+        outer, inner, cores = spot.sizes
+        self.part = width // cores
+        self.half = self.part // 2
+        self.own = self.half // (outer * inner)
+        self.base = (spot.core * self.part, spot.core * self.part + self.half)
+        a_big, b_big = self.half // inner, self.half // outer
+        self.big = (a_big, b_big)
+        self.first = ("inner", "outer")
+        place = {"inner": spot.inner, "outer": spot.outer}
+        size = {"inner": inner, "outer": outer}
+        self.lines = tuple(Line(spot, name, size[name], place[name]) for name in ("inner", "outer"))
+        self.offset = (
+            spot.inner * a_big + spot.outer * self.own,
+            spot.outer * b_big + spot.inner * self.own,
+        )
+        self.group = (spot.inner * a_big, spot.outer * b_big)
+
+    def order(self, path):
+        return (self.lines[0], self.lines[1]) if path == 0 else (self.lines[1], self.lines[0])
+
+
+def rows_at(ref, start, count):
+    return ref.at[:, pl.ds(pl.multiple_of(start, 8), count), :]
+
+
+def reduce_kernel(
+    shape, modes, width, grad_ref, illum_ref, dir_ref, pre_ref, sums_ref,
+    held, held_i, prev, shift_in, shift_all, sums_in, sums_all, *rest,
+):
+    outer, inner, cores = shape
+    spot = Spot(outer, inner, cores)
+    share = Shares(spot, width)
+    (slots, islots, core_s, core_r, sc_s, sc_r, ga_s, ga_r, isc_s, isc_r, back_s, back_r, dir_sem, bc_s, bc_r) = (
+        rest[0:4], rest[4:8], *rest[8:10], rest[10:14], rest[14:18], rest[18:22], rest[22:26],
+        rest[26:30], rest[30:34], *rest[34:],
+    )
+    me, count = spot.me, spot.count
+    pixels = float(width * width)
+
+    barrier = pltpu.get_barrier_semaphore()
+    for step in range(1, count):
+        pl.semaphore_signal(barrier, inc=1, device_id={"grp": lax.rem(me + step, count)}, device_id_type=MESH)
+
+    loads = []
+    for path in range(2):
+        start = pl.multiple_of(share.base[path] + share.offset[path], 8)
+        for m in range(modes):
+            load = pltpu.make_async_copy(
+                dir_ref.at[:, m, pl.ds(start, share.own), :], prev.at[path, m], dir_sem.at[path, m]
+            )
+            load.start()
+            loads.append(load)
+    pl.semaphore_wait(barrier, count - 1)
+
+    def core_send(src, dst, item):
+        return remote(src, dst, core_s.at[item], core_r.at[item], spot.partner())
+
+    def partial(m):
+        return grad_ref.at[m] if m < modes else illum_ref
+
+    def keep(m):
+        return held.at[m] if m < modes else held_i
+
+    def give(m):
+        other = (1 - spot.core) * share.part
+        return core_send(rows_at(partial(m), other, share.part), keep(m), m)
+
+    items = [modes] + list(range(modes))
+    for m in items:
+        give(m).start()
+
+    def pair(m, path):
+        if m < modes:
+            one, two = 2 * path, 2 * path + 1
+            return [(slots[k].at[m], sc_s[k].at[m], sc_r[k].at[m]) for k in (one, two)]
+        return [(islots[k], isc_s[k], isc_r[k]) for k in (2 * path, 2 * path + 1)]
+
+    def scatter_parts(m, path):
+        first, second = share.order(path)
+        at = path * share.half
+        top = lambda k: rows_at(keep(m), at + k * share.big[path], share.big[path])
+        low = lambda k: rows_at(keep(m), at + share.group[path] + k * share.own, share.own)
+        return [(line, chunk) + sems for line, chunk, sems in zip((first, second), (top, low), pair(m, path))]
+
+    def gather_parts(m, path):
+        second, first = share.order(path)
+        base = share.base[path]
+        low = lambda k: rows_at(pre_ref.at[m], base + share.group[path] + k * share.own, share.own)
+        top = lambda k: rows_at(pre_ref.at[m], base + k * share.big[path], share.big[path])
+        sems = [(ga_s[k].at[m], ga_r[k].at[m]) for k in (2 * path, 2 * path + 1)]
+        return [(line, chunk) + pairs for line, chunk, pairs in zip((first, second), (low, top), sems)]
+
+    def home(m, path):
+        block = rows_at(pre_ref.at[m], share.base[path], share.half)
+        return remote(block, block, back_s.at[m, path], back_r.at[m, path], spot.partner())
+
+    def broadcast(src, dst, which):
+        copies = []
+        for step in range(1, count):
+            to = lax.rem(me + step, count)
+            copies.append(remote(src, dst.at[step], bc_s.at[which, step], bc_r.at[which, step], {"grp": to}))
+        return copies
+
+    def own_illum(path):
+        at = pl.multiple_of(path * share.half + share.offset[path], 8)
+        return held_i[0, pl.ds(at, share.own), :]
+
+    def scatter(m, path):
+        if path == 0:
+            give(m).wait_recv()
+            held_m, mine = keep(m), partial(m)
+            step = 32 if share.part % 32 == 0 else share.part
+
+            def add(i, carry):
+                rows = pl.ds(pl.multiple_of(i * step, 8), step)
+                held_m[:, rows, :] += mine[:, pl.ds(pl.multiple_of(spot.core * share.part + i * step, 8), step), :]
+                return carry
+
+            lax.fori_loop(0, share.part // step, add, 0)
+        for line, chunk, slot, send, recv in scatter_parts(m, path):
+            yield from line.scatter(chunk, slot, send, recv)
+
+    def illum_done():
+        tile = fold_lanes(own_illum(0)) + fold_lanes(own_illum(1))
+        shift_in[...] = tile
+        for copy in broadcast(shift_in, shift_all, 0):
+            copy.start()
+        shift_all[0] = tile
+
+    def shift_value():
+        for copy in broadcast(shift_in, shift_all, 0):
+            copy.wait_recv()
+        return jnp.sum(shift_all[...]) / pixels
+
+    def mode(m, path, shift):
+        yield from scatter(m, path)
+        at = pl.multiple_of(path * share.half + share.offset[path], 8)
+        rows = pl.ds(at, share.own)
+        to = pl.ds(pl.multiple_of(share.base[path] + share.offset[path], 8), share.own)
+        light = own_illum(path)
+        loads[path * modes + m].wait()
+        g_re, g_im = held[m, 0, rows, :], held[m, 1, rows, :]
+        d_re, d_im = prev[path, m, 0], prev[path, m, 1]
+        den = light + shift
+        p_re, p_im = g_re / den, g_im / den
+        pre_ref[m, 0, to, :] = p_re
+        pre_ref[m, 1, to, :] = p_im
+        parts = gather_parts(m, path)
+        line, chunk, send, recv = parts[0]
+        walk = line.gather(chunk, send, recv)
+        next(walk, None)
+        terms = (
+            g_re * p_re + g_im * p_im,
+            g_re * d_re + g_im * d_im,
+            light * (p_re * p_re + p_im * p_im),
+            light * (p_re * d_re + p_im * d_im),
+            light * (d_re * d_re + d_im * d_im),
+        )
+        for k, term in enumerate(terms):
+            tile = jnp.sum(fold_lanes(term), axis=0, keepdims=True)
+            row = 5 * m + k
+            sums_in[row : row + 1, :] = tile if path == 0 else sums_in[row : row + 1, :] + tile
+        yield
+        yield from walk
+        line, chunk, send, recv = parts[1]
+        yield from line.gather(chunk, send, recv)
+        home(m, path).start()
+
+    def run(streams):
+        streams = list(streams)
+        while streams:
+            alive = []
+            for stream in streams:
+                try:
+                    next(stream)
+                    alive.append(stream)
+                except StopIteration:
+                    pass
+            streams = alive
+
+    sums_in[...] = jnp.zeros_like(sums_in)
+    run([scatter(modes, 0), scatter(modes, 1)])
+    illum_done()
+    shift = shift_value()
+
+    def lagged(stream, lag):
+        for _ in range(lag):
+            yield
+        yield from stream
+
+    run(lagged(mode(m, path, shift), 2 * m) for m in range(modes) for path in range(2))
+
+    for copy in broadcast(sums_in, sums_all, 1):
+        copy.start()
+    sums_all[0] = sums_in[...]
+    for copy in broadcast(sums_in, sums_all, 1):
+        copy.wait_recv()
+    sums_ref[...] = jnp.sum(sums_all[...], axis=0)
+
+    for m in range(modes):
+        for path in range(2):
+            home(m, path).wait_recv()
+    for m in items:
+        give(m).wait_send()
+        for path in range(2):
+            for line, chunk, slot, send, recv in scatter_parts(m, path):
+                line.scatter_end(chunk, slot, send, recv)
+            if m < modes:
+                for line, chunk, send, recv in gather_parts(m, path):
+                    line.gather_end(chunk, send, recv)
+                home(m, path).wait_send()
+    for which, src, dst in ((0, shift_in, shift_all), (1, sums_in, sums_all)):
+        for copy in broadcast(src, dst, which):
+            copy.wait_send()
+
+
+def reduce_grads(part, illum, direction):
+    modes, _, width, _ = part.shape
+    shape = split_lines(lax.axis_size("grp"))
+    outer, inner, cores = shape
+    count = outer * inner * cores
+    half = width // cores // 2
+    own = half // (outer * inner)
+    sizes = [(inner, half // inner), (outer, own), (outer, half // outer), (inner, own)]
+    back_sizes = [outer, inner, inner, outer]
+    sum_rows = -(-5 * modes // 8) * 8
+    lanes = min(128, width)
+    dma = pltpu.SemaphoreType.DMA
+    f32 = jnp.float32
+    scratch = [
+        pltpu.VMEM((modes, 2, width // cores, width), f32),
+        pltpu.VMEM((1, width // cores, width), f32),
+        pltpu.VMEM((2, modes, 2, own, width), f32),
+        pltpu.VMEM((8, lanes), f32),
+        pltpu.VMEM((count, 8, lanes), f32),
+        pltpu.VMEM((sum_rows, lanes), f32),
+        pltpu.VMEM((count, sum_rows, lanes), f32),
+    ]
+    scratch += [pltpu.VMEM((modes, n + 1, 2, rows, width), f32) for n, rows in sizes]
+    scratch += [pltpu.VMEM((n + 1, 1, rows, width), f32) for n, rows in sizes]
+    scratch += [dma((modes + 1,)), dma((modes + 1,))]
+    scratch += [dma((modes, n)) for n, _ in sizes] + [dma((modes, n + 1)) for n, _ in sizes]
+    scratch += [dma((modes, 2, n)) for n in back_sizes] + [dma((modes, n)) for n in back_sizes]
+    scratch += [dma((n,)) for n, _ in sizes] + [dma((n + 1,)) for n, _ in sizes]
+    scratch += [dma((modes, 2)), dma((modes, 2)), dma((2, modes)), dma((2, count)), dma((2, count))]
+    vmem = pl.BlockSpec(memory_space=pltpu.VMEM)
+    return pl.pallas_call(
+        functools.partial(reduce_kernel, shape, modes, width),
+        in_specs=[vmem, vmem, pl.BlockSpec(memory_space=pl.ANY)],
+        out_specs=[vmem, vmem],
+        out_shape=[
+            jax.ShapeDtypeStruct(part.shape, f32),
+            jax.ShapeDtypeStruct((sum_rows, lanes), f32),
+        ],
+        scratch_shapes=scratch,
+        compiler_params=pltpu.CompilerParams(collective_id=0, has_side_effects=True, vmem_limit_bytes=VMEM_LIMIT),
+        name="reduce",
+    )(part, illum[None], direction)
+
+
+def finish_kernel(norm_ref, sums_ref, pre_ref, probe_ref, dir_ref, new_probe, new_dir, new_norm):
+    mode = pl.program_id(0)
+    pixels = float(new_probe.shape[3] ** 2)
+    index = lax.broadcasted_iota(jnp.int32, sums_ref.shape, 0)
+
+    def mean(k):
+        return jnp.sum(jnp.where(index == 5 * mode + k, sums_ref[...], 0.0)) / pixels
+
+    norm, cross, light, light_cross, light_prev = (mean(k) for k in range(5))
+    new_norm[mode] = norm
+    beta = norm / norm_ref[mode]
+    upper = norm + beta * cross
+    lower = light + beta * (2.0 * light_cross + beta * light_prev)
+    alpha = upper / (lower + 1.0)
+    for part in range(2):
+        step = pre_ref[0, part] + beta * dir_ref[part, 0]
+        new_dir[part, 0] = step
+        new_probe[part, 0] = probe_ref[part, 0] + alpha * step
+
+
+def finish(prev_norm, sums, pre, probe, direction):
+    modes, width = probe.shape[1], probe.shape[2]
+    rows = min(128, width)
+    block = pl.BlockSpec((2, 1, rows, width), lambda m, r: (0, m, r, 0))
+    smem = pl.BlockSpec(memory_space=pltpu.SMEM)
     return pl.pallas_call(
         finish_kernel,
-        grid=(modes,),
+        grid=(modes, width // rows),
         in_specs=[
-            pl.BlockSpec(memory_space=pltpu.SMEM),
-            pl.BlockSpec((1, 2, width, width), lambda m: (m, 0, 0, 0)),
-            whole(illum.shape),
+            smem,
+            whole(sums.shape),
+            pl.BlockSpec((1, 2, rows, width), lambda m, r: (m, 0, r, 0)),
             block,
             block,
         ],
-        out_specs=[block, block, pl.BlockSpec(memory_space=pltpu.SMEM)],
+        out_specs=[block, block, smem],
         out_shape=[
             jax.ShapeDtypeStruct(probe.shape, jnp.float32),
             jax.ShapeDtypeStruct(probe.shape, jnp.float32),
             jax.ShapeDtypeStruct((modes,), jnp.float32),
         ],
-        compiler_params=params(),
+        compiler_params=pltpu.CompilerParams(
+            dimension_semantics=("arbitrary", "arbitrary"), vmem_limit_bytes=32 * 1024 * 1024
+        ),
         name="finish",
-    )(prev_norm, grad, illum, probe, direction)
+    )(prev_norm, sums, pre, probe, direction)
 
 
 def sum_over_modes(local_sum):
@@ -315,8 +685,8 @@
         grad = backward(base, total, amplitude, index, wave, exits, patches[index], grad, 0, modes)
     wave, exits, total = kept[-1]
     part = backward(base, total, amplitude, positions - 1, wave, exits, patches[-1], grad, 0, modes)
-    part, illum = lax.psum((part, illum), "grp")
-    return tuple(finish(prev_norm, part, illum, probe, prev_direction))
+    pre, sums = reduce_grads(part, illum, prev_direction)
+    return tuple(finish(prev_norm, sums, pre, probe, prev_direction))
 
 
 def solution(mesh):

time: 322 us -> 295 us (0.916)
  waiting for transfers between devices: 190 us -> 3.99 us
  Pallas kernels: 90.1 us -> 255 us
  between operations: 21.8 us -> 8.42 us
  local copies, waits for them, and re-layouts: 1.45 us -> 8.92 us
    psum x1 -> x0, waiting for transfers between devices: 186 us -> none  [on_device(): part, illum = lax.psum((part, illum), 'grp')]
    pallas_call x1 -> x2, Pallas kernels: 16.5 us -> 181 us  [the longest x1 165 us: reduce_grads(): pl.pallas_call(functools.partial(reduce_kernel, shape, modes, width), in_...]
    unnamed x6 -> x14, local copies, waits for them, and re-layouts: 0.01 us -> 7.48 us
  transfers between devices with their start and end apart: 3 -> 2, of which waited for: 3 -> 2; matrix products, arithmetic and copies ran while one was open for 2% -> 2% of each run, Pallas kernels for 11% -> 12%
where the time goes in v1:
time: 295 us; the launch traced here: 294 us
  Pallas kernels  255 us (86%)
  other arithmetic  15.4 us (5%)
  local copies, waits for them, and re-layouts  8.92 us (3%)
  between operations  8.42 us (3%)
  waiting for transfers between devices  3.99 us (1%)
  starting transfers between devices  3.16 us (1%)
    pallas_call x1, Pallas kernels, reduce_grads(): pl.pallas_call(functools.partial(reduce_kernel, shape, modes, width), in_...  165 us
    pallas_call x2, Pallas kernels, backward(): pl.pallas_call(functools.partial(backward_kernel, grad is None), grid=(co...  37.8 us
    pallas_call x2, Pallas kernels, forward(): pl.pallas_call(forward_kernel, grid=(modes,), in_specs=[whole(base.shape)...  35.8 us
    pallas_call x1, Pallas kernels, finish(): pl.pallas_call(finish_kernel, grid=(modes, width // rows), in_specs=[smem...  15.5 us
    unnamed x14, local copies, waits for them, and re-layouts  7.48 us
  transfers between devices with their start and end apart: 2, of which 2 were waited for; matrix products, arithmetic and copies ran while one was open for 2% of the time, Pallas kernels for 12%

profile of v1, /device:TPU:0, one launch (start us, length us, event | category | flops | bytes accessed | tf_op | source)
XLA Modules:
  0.0 294.5 jit_solution(1286634414981337536)
XLA Ops:
  0.6 0.0 copy-start.4
  0.6 1.4 fusion.11
  7.2 4.4 %multiply_convert_fusion = (bf16[1,512,512]{2,1,0:T(8,128)(2,1)S(1)}, bf16[1,512,512]{2,1,0:T(8,128)(2,1)S(1)}) fusion(), kind=kLoop, calls=%fused_computation.14 | loop fusion | flops 4718592 | bytes 1048576 | tf_op jit(solution)/shard_map/convert_element_type | solution.py:22
  14.2 1.1 pad_maximum_fusion.base_ref
  15.3 0.0 copy-done.4
  15.3 3.2 %fusion.9 = (f32[2,512,512]{2,1,0:T(8,128)S(1)}, bf16[2,512,512]{2,1,0:T(8,128)(2,1)}, f32[2,512,512]{2,1,0:T(8,128)}, bf16[2,512,512]{2,1,0:T(8,128)(2,1)}) fusion(bf16[2,640,640]{2,1,0:T(8,128)(2,1)S(1)} %copy-done.4, s32[]{:T(128)S(6)} %select_n.35, s32[]{:T(128)S(6)} %select_n.36, s32[]{:T(128)S(6)} %select_n.33, s32[]{:T(128)S(6)} %select_n.34), kind=kLoop, calls=%fused_computation.21 | loop fusion | flops 1048576 | bytes 8388624 | tf_op jit(solution)/shard_map/convert_element_type | solution.py:680
  18.5 17.9 %forward.3 = (f32[4,2,512,512]{3,2,1,0:T(8,128)}, bf16[4,2,512,512]{3,2,1,0:T(8,128)(2,1)}, f32[512,512]{1,0:T(8,128)}) custom-call(bf16[2,512,512]{2,1,0:T(8,128)(2,1)} %pad_maximum_fusion.base_ref, f32[2,4,512,512]{3,2,1,0:T(8,128)} %probe_ref.5, bf16[2,512,512]{2,1,0:T(8,128)(2,1)} %get-tuple-element.20.patch_ref), custom_call_target="tpu_custom_call" | custom-call | flops 8589934592 | bytes 20971520 | tf_op jit(solution)/shard_map/forward/pallas_call | solution.py:285
  36.4 3.1 %collective-permute-start.1 = (f32[512,512]{1,0:T(8,128)}, f32[512,512]{1,0:T(8,128)}, u32[]{:S(2)}, u32[]{:S(2)}) collective-permute-start(f32[512,512]{1,0:T(8,128)} %get-tuple-element.14), channel_id=1, source_target_pairs={{0,1},{1,0},{2,3},{3,2},{4,5},{5,4},{6,7},{7,6},{8,9},{9,8},{10,11... | collective-permute-start | bytes 3145736 | tf_op jit(solution)/shard_map/ppermute | solution.py:662
  39.4 17.9 %forward.2 = (f32[4,2,512,512]{3,2,1,0:T(8,128)}, bf16[4,2,512,512]{3,2,1,0:T(8,128)(2,1)}, f32[512,512]{1,0:T(8,128)}) custom-call(bf16[2,512,512]{2,1,0:T(8,128)(2,1)} %pad_maximum_fusion.base_ref, f32[2,4,512,512]{3,2,1,0:T(8,128)} %probe_ref.5, bf16[2,512,512]{2,1,0:T(8,128)(2,1)} %get-tuple-element.24.patch_ref), custom_call_target="tpu_custom_call" | custom-call | flops 8589934592 | bytes 20971520 | tf_op jit(solution)/shard_map/forward/pallas_call | solution.py:285
  57.4 0.0 copy-start.6
  57.4 0.1 collective-permute-start
  57.5 3.1 %fusion.3.illum_ref = f32[1,512,512]{2,1,0:T(8,128)} fusion(f32[2,512,512]{2,1,0:T(8,128)} %get-tuple-element.23, f32[2,512,512]{2,1,0:T(8,128)S(1)} %get-tuple-element.19), kind=kLoop, calls=%fused_computation.7 | loop fusion | flops 1835008 | bytes 5242880 | tf_op jit(solution)/shard_map/add | solution.py:681
  60.6 3.2 %collective-permute-done.1 = f32[512,512]{1,0:T(8,128)} collective-permute-done((f32[512,512]{1,0:T(8,128)}, f32[512,512]{1,0:T(8,128)}, u32[]{:S(2)}, u32[]{:S(2)}) %collective-permute-start.1) | collective-permute-done | bytes 1048608 | tf_op jit(solution)/shard_map/ppermute | solution.py:662
  63.8 0.0 copy-done.6
  63.8 2.4 add.55.total_ref
  66.2 0.0 copy-start.5
  66.2 18.3 %backward.2.rest_0_ = f32[4,2,512,512]{3,2,1,0:T(8,128)} custom-call(bf16[2,512,512]{2,1,0:T(8,128)(2,1)} %pad_maximum_fusion.base_ref, f32[512,512]{1,0:T(8,128)} %add.55.total_ref, bf16[2,512,512]{2,1,0:T(8,128)(2,1)} %amp_ref.3, f32[4,2,512,512]{3,2,1,0:T(8,128)} %get-tuple-element.15.wave_ref, bf16[4,2,512,512]{3,2,1,0:T(8,128)(2,1)} %get-tuple-element.16.exit_ref, ...), custom_call_target="tpu_custom_call" | custom-call | flops 8589934592 | bytes 25165824 | tf_op jit(solution)/shard_map/backward/pallas_call | solution.py:326
  84.5 0.8 collective-permute-done
  85.3 0.0 copy-done.5
  85.3 1.3 add.52.total_ref
  86.6 19.4 %backward.3.grad_ref = f32[4,2,512,512]{3,2,1,0:T(8,128)} custom-call(bf16[2,512,512]{2,1,0:T(8,128)(2,1)} %pad_maximum_fusion.base_ref, f32[512,512]{1,0:T(8,128)} %add.52.total_ref, bf16[2,512,512]{2,1,0:T(8,128)(2,1)} %amp_ref.3, f32[4,2,512,512]{3,2,1,0:T(8,128)} %get-tuple-element.12.wave_ref, bf16[4,2,512,512]{3,2,1,0:T(8,128)(2,1)} %get-tuple-element.13.exit_ref, ...), custom_call_target="tpu_custom_call" | custom-call | flops 8589934592 | bytes 25165824 | tf_op jit(solution)/shard_map/backward/pallas_call | solution.py:326
  106.0 0.0 copy-start.3
  106.0 165.5 %reduce.1 = (f32[4,2,512,512]{3,2,1,0:T(8,128)}, f32[24,128]{1,0:T(8,128)}) custom-call(f32[4,2,512,512]{3,2,1,0:T(8,128)} %backward.3.grad_ref, f32[1,512,512]{2,1,0:T(8,128)} %fusion.3.illum_ref, f32[2,4,512,512]{3,2,1,0:T(8,128)} %dir_ref.3), custom_call_target="tpu_custom_call" | custom-call | tf_op jit(solution)/shard_map/reduce/pallas_call | solution.py:597
  271.5 0.0 copy-done.3
  271.5 0.0 copy-start
  271.5 3.4 %copy-done = f32[2,4,512,512]{3,2,1,0:T(8,128)S(1)} copy-done((f32[2,4,512,512]{3,2,1,0:T(8,128)S(1)}, f32[2,4,512,512]{3,2,1,0:T(8,128)}, u32[]{:S(2)}) %copy-start) | copy-done | bytes 8388632
  274.9 0.0 copy-start.1
  274.9 3.4 %copy-done.1 = f32[4,2,512,512]{3,2,1,0:T(8,128)S(1)} copy-done((f32[4,2,512,512]{3,2,1,0:T(8,128)S(1)}, f32[4,2,512,512]{3,2,1,0:T(8,128)}, u32[]{:S(2)}) %copy-start.1) | copy-done | bytes 8388632
  278.3 0.0 copy-start.2
  278.3 0.7 copy-done.2
  279.0 15.5 %finish.1 = (f32[2,4,512,512]{3,2,1,0:T(8,128)}, f32[2,4,512,512]{3,2,1,0:T(8,128)}, f32[4]{0:T(128)}) custom-call(f32[4]{0:T(128)S(1)} %copy-done.3, f32[24,128]{1,0:T(8,128)S(1)} %copy-done.2, f32[4,2,512,512]{3,2,1,0:T(8,128)S(1)} %copy-done.1, f32[2,4,512,512]{3,2,1,0:T(8,128)S(1)} %copy-done, f32[2,4,512,512]{3,2,1,0:T(8,128)} %dir_ref.3), custom_call_target="tpu_custom_call" | custom-call | tf_op jit(solution)/shard_map/finish/pallas_call | solution.py:636
Async XLA Ops:
  0.6 14.7 %copy-start.4 = (bf16[2,640,640]{2,1,0:T(8,128)(2,1)S(1)}, bf16[2,640,640]{2,1,0:T(8,128)(2,1)}, u32[]{:S(2)}) copy-start(bf16[2,640,640]{2,1,0:T(8,128)(2,1)} %param.9) | copy-start | bytes 4915204
  36.4 27.4 %collective-permute-start.1 = (f32[512,512]{1,0:T(8,128)}, f32[512,512]{1,0:T(8,128)}, u32[]{:S(2)}, u32[]{:S(2)}) collective-permute-start(f32[512,512]{1,0:T(8,128)} %get-tuple-element.14), channel_id=1, source_target_pairs={{0,1},{1,0},{2,3},{3,2},{4,5},{5,4},{6,7},{7,6},{8,9},{9,8},{10,11... | collective-permute-start | bytes 3145736 | tf_op jit(solution)/shard_map/ppermute | solution.py:662
  57.4 6.4 %copy-start.6 = (f32[512,512]{1,0:T(8,128)S(1)}, f32[512,512]{1,0:T(8,128)}, u32[]{:S(2)}) copy-start(f32[512,512]{1,0:T(8,128)} %get-tuple-element.14) | copy-start | bytes 3145732
  57.4 28.0 %collective-permute-start = (f32[512,512]{1,0:T(8,128)}, f32[512,512]{1,0:T(8,128)S(1)}, u32[]{:S(2)}, u32[]{:S(2)}) collective-permute-start(f32[512,512]{1,0:T(8,128)} %get-tuple-element.11), channel_id=1, source_target_pairs={{0,1},{1,0},{2,3},{3,2},{4,5},{5,4},{6,7},{7,6},{8,9},{9,8},{10,11... | collective-permute-start | bytes 3145736 | tf_op jit(solution)/shard_map/ppermute | solution.py:662
  66.2 19.1 %copy-start.5 = (f32[512,512]{1,0:T(8,128)S(1)}, f32[512,512]{1,0:T(8,128)}, u32[]{:S(2)}) copy-start(f32[512,512]{1,0:T(8,128)} %get-tuple-element.11) | copy-start | bytes 3145732
  106.0 165.5 %copy-start.3 = (f32[4]{0:T(128)S(1)}, f32[4]{0:T(128)}, u32[]{:S(2)}) copy-start(f32[4]{0:T(128)} %norm_ref.1) | copy-start | bytes 52
  271.5 3.4 %copy-start = (f32[2,4,512,512]{3,2,1,0:T(8,128)S(1)}, f32[2,4,512,512]{3,2,1,0:T(8,128)}, u32[]{:S(2)}) copy-start(f32[2,4,512,512]{3,2,1,0:T(8,128)} %probe_ref.5) | copy-start | bytes 25165828
  274.9 3.4 %copy-start.1 = (f32[4,2,512,512]{3,2,1,0:T(8,128)S(1)}, f32[4,2,512,512]{3,2,1,0:T(8,128)}, u32[]{:S(2)}) copy-start(f32[4,2,512,512]{3,2,1,0:T(8,128)} %get-tuple-element.18.pre_ref) | copy-start | bytes 25165828
  278.3 0.7 copy-start.2

commit v2 on v1

--- a/solution.py
+++ b/solution.py
@@ -10,7 +10,7 @@
 
 MESH = pl.DeviceIdType.MESH
 VMEM_LIMIT = 60 * 1024 * 1024
-TILE = 256
+FRONT_LIMIT = 67043328
 
 
 def base_table(width):
@@ -21,116 +21,6 @@
     real_part = (jnp.cos(angle) * scale).astype(jnp.bfloat16)
     imag_part = (jnp.sin(angle) * scale).astype(jnp.bfloat16)
     return jnp.stack([real_part, imag_part])
-
-
-def build_pair(base_ref, plus, minus):
-    width = base_ref.shape[1]
-    cosine, sine = base_ref[0], base_ref[1]
-    for ref, sign in ((plus, 1), (minus, -1)):
-        ref[:width, :width] = cosine
-        ref[width:, width:] = cosine
-        ref[:width, width:] = sine if sign > 0 else -sine
-        ref[width:, :width] = -sine if sign > 0 else sine
-
-
-def transform(joined, stacked, right, left, emit):
-    width = joined.shape[0]
-    tile = min(TILE, width)
-
-    def first(step, carry):
-        at = pl.multiple_of(step * tile, tile)
-        half = jnp.dot(joined[pl.ds(at, tile), :], right[...], preferred_element_type=jnp.float32)
-        half = half.astype(jnp.bfloat16)
-        stacked[pl.ds(at, tile), :] = half[:, :width]
-        stacked[pl.ds(at + width, tile), :] = half[:, width:]
-        return carry
-
-    def second(step, carry):
-        at = pl.multiple_of(step * tile, tile)
-        rows = pl.ds(at, tile)
-        real = jnp.dot(left[rows, :], stacked[...], preferred_element_type=jnp.float32)
-        imag = jnp.dot(left[pl.ds(at + width, tile), :], stacked[...], preferred_element_type=jnp.float32)
-        emit(rows, real, imag)
-        return carry
-
-    lax.fori_loop(0, width // tile, first, 0)
-    lax.fori_loop(0, width // tile, second, 0)
-
-
-def forward_kernel(base_ref, probe_ref, patch_ref, wave_ref, exit_ref, sum_ref, plus, minus, joined, stacked):
-    mode = pl.program_id(0)
-    width = sum_ref.shape[0]
-    tile = 64
-
-    @pl.when(mode == 0)
-    def _():
-        build_pair(base_ref, plus, minus)
-        sum_ref[...] = jnp.zeros_like(sum_ref)
-
-    def leave(step, carry):
-        rows = pl.ds(pl.multiple_of(step * tile, tile), tile)
-        obj_re = patch_ref[0, rows, :].astype(jnp.float32)
-        obj_im = patch_ref[1, rows, :].astype(jnp.float32)
-        pro_re, pro_im = probe_ref[0, 0, rows, :], probe_ref[1, 0, rows, :]
-        exit_re = (pro_re * obj_re - pro_im * obj_im).astype(jnp.bfloat16)
-        exit_im = (pro_re * obj_im + pro_im * obj_re).astype(jnp.bfloat16)
-        joined[rows, :width] = exit_re
-        joined[rows, width:] = exit_im
-        exit_ref[0, 0, rows, :] = exit_re
-        exit_ref[0, 1, rows, :] = exit_im
-        return carry
-
-    lax.fori_loop(0, width // tile, leave, 0)
-
-    def emit(rows, real, imag):
-        wave_ref[0, 0, rows, :] = real
-        wave_ref[0, 1, rows, :] = imag
-        sum_ref[rows, :] += real * real + imag * imag
-
-    transform(joined, stacked, plus, minus, emit)
-
-
-def backward_kernel(first, base_ref, total_ref, amp_ref, wave_ref, exit_ref, patch_ref, *rest):
-    if first:
-        grad_in, (grad_ref, plus, minus, joined, stacked, ratio) = None, rest
-    else:
-        grad_in, grad_ref, plus, minus, joined, stacked, ratio = rest
-    width = total_ref.shape[0]
-    tile = 64
-
-    @pl.when(pl.program_id(0) == 0)
-    def _():
-        build_pair(base_ref, plus, minus)
-
-        def scale(step, carry):
-            rows = pl.ds(pl.multiple_of(step * tile, tile), tile)
-            ratio[rows, :] = amp_ref[0, rows, :].astype(jnp.float32) / jnp.sqrt(total_ref[rows, :] + 1.0)
-            return carry
-
-        lax.fori_loop(0, width // tile, scale, 0)
-
-    def fix(step, carry):
-        rows = pl.ds(pl.multiple_of(step * tile, tile), tile)
-        joined[rows, :width] = (ratio[rows, :] * wave_ref[0, 0, rows, :]).astype(jnp.bfloat16)
-        joined[rows, width:] = (ratio[rows, :] * wave_ref[0, 1, rows, :]).astype(jnp.bfloat16)
-        return carry
-
-    lax.fori_loop(0, width // tile, fix, 0)
-
-    def emit(rows, real, imag):
-        obj_re = patch_ref[0, rows, :].astype(jnp.float32)
-        obj_im = patch_ref[1, rows, :].astype(jnp.float32)
-        diff_re = real - exit_ref[0, 0, rows, :].astype(jnp.float32)
-        diff_im = imag - exit_ref[0, 1, rows, :].astype(jnp.float32)
-        add_re = obj_re * diff_re + obj_im * diff_im
-        add_im = obj_re * diff_im - obj_im * diff_re
-        if grad_in is not None:
-            add_re = grad_in[0, 0, rows, :] + add_re
-            add_im = grad_in[0, 1, rows, :] + add_im
-        grad_ref[0, 0, rows, :] = add_re
-        grad_ref[0, 1, rows, :] = add_im
-
-    transform(joined, stacked, minus, plus, emit)
 
 
 def fold_lanes(block):
@@ -259,81 +149,195 @@
                     remote(chunk(k), chunk(k), send.at[way, k], recv.at[k], self.spot.at(self.name, 0)).wait_send()
 
 
-def whole(shape):
-    return pl.BlockSpec(shape, lambda *_: (0,) * len(shape))
-
-
-def table_scratch(width):
-    return [
-        pltpu.VMEM((2 * width, 2 * width), jnp.bfloat16),
-        pltpu.VMEM((2 * width, 2 * width), jnp.bfloat16),
-        pltpu.VMEM((width, 2 * width), jnp.bfloat16),
-        pltpu.VMEM((2 * width, width), jnp.bfloat16),
-    ]
-
-
-def params():
-    return pltpu.CompilerParams(dimension_semantics=("arbitrary",), vmem_limit_bytes=VMEM_LIMIT)
-
-
-def cost(modes, width, moved):
-    return pl.CostEstimate(flops=modes * 16 * width**3, bytes_accessed=moved, transcendentals=0)
-
-
-def forward(base, probe, patch):
+def build_tables(base_ref, plus, minus):
+    width = base_ref.shape[1]
+    tile = width // 2
+    for row in range(2):
+        for col in range(2):
+            take = (pl.ds(row * tile, tile), pl.ds(col * tile, tile))
+            cosine, sine = base_ref[(0, *take)], base_ref[(1, *take)]
+            for ref, upper, lower in ((plus, sine, -sine), (minus, -sine, sine)):
+                r, c = row * width, col * width
+                ref[r : r + tile, c : c + tile] = cosine
+                ref[r + tile : r + width, c + tile : c + width] = cosine
+                ref[r : r + tile, c + tile : c + width] = upper
+                ref[r + tile : r + width, c : c + tile] = lower
+
+
+def front_kernel(
+    peers, base_ref, probe_ref, patch_ref, amp_ref, grad_ref,
+    plus, minus, probe, exits, wave, stacked, own, other, load_sem, send_sem, recv_sem,
+):
+    positions, modes = exits.shape[0], exits.shape[1]
+    width = base_ref.shape[1]
+    tile = width // 2
+    step = min(64, tile)
+    f32, bf16 = jnp.float32, jnp.bfloat16
+    y = lax.axis_index("mode")
+
+    barrier = pltpu.get_barrier_semaphore()
+    for k in range(1, peers):
+        pl.semaphore_signal(barrier, inc=1, device_id={"mode": lax.rem(y + k, peers)}, device_id_type=MESH)
+
+    def load(m):
+        return pltpu.make_async_copy(probe_ref.at[:, m], probe.at[m], load_sem.at[m])
+
+    for m in range(modes):
+        load(m).start()
+    build_tables(base_ref, plus, minus)
+    if peers > 1:
+        pl.semaphore_wait(barrier, peers - 1)
+
+    def swap(p, t, k):
+        rows = pl.ds(t * tile, tile)
+        return remote(
+            own.at[p, rows], other.at[k - 1, p, rows], send_sem.at[k - 1, p, t], recv_sem.at[k - 1, p, t],
+            {"mode": lax.rem(y + k, peers)},
+        )
+
+    def put(half, m, rows):
+        for col in range(2):
+            for part in range(2):
+                block = half[:, (2 * col + part) * tile : (2 * col + part + 1) * tile]
+                stacked[m, pl.ds(rows * width + part * tile, tile), col * tile : (col + 1) * tile] = block
+
+    def leave(p, m):
+        def body(i, carry):
+            rows = pl.ds(pl.multiple_of(i * step, step), step)
+            for col in range(2):
+                at = pl.ds(col * tile, tile)
+                obj_re = patch_ref[p, 0, rows, at].astype(f32)
+                obj_im = patch_ref[p, 1, rows, at].astype(f32)
+                pro_re, pro_im = probe[m, 0, rows, at], probe[m, 1, rows, at]
+                exits[p, m, rows, 2 * col * tile : (2 * col + 1) * tile] = (pro_re * obj_re - pro_im * obj_im).astype(bf16)
+                exits[p, m, rows, (2 * col + 1) * tile : (2 * col + 2) * tile] = (pro_re * obj_im + pro_im * obj_re).astype(bf16)
+            return carry
+
+        lax.fori_loop(0, width // step, body, 0)
+
+    def forward(p, carry):
+        def first(m, carry):
+            @pl.when(p == 0)
+            def _():
+                load(m).wait()
+
+            leave(p, m)
+            half = jnp.dot(exits[p, m], plus[...], preferred_element_type=f32).astype(bf16)
+            for rows in range(2):
+                put(half[rows * tile : (rows + 1) * tile], m, rows)
+            return carry
+
+        lax.fori_loop(0, modes, first, 0)
+        for t in range(2):
+            rows = pl.ds(t * tile, tile)
+
+            def second(m, carry):
+                out = jnp.dot(minus[t * width : (t + 1) * width, :], stacked[m], preferred_element_type=f32)
+                real, imag = out[:tile], out[tile:]
+                wave[p, m, t, 0] = real
+                wave[p, m, t, 1] = imag
+                light = real * real + imag * imag
+                own[p, rows, :] = jnp.where(m == 0, light, own[p, rows, :] + light)
+                return carry
+
+            lax.fori_loop(0, modes, second, 0)
+            for k in range(1, peers):
+                swap(p, t, k).start()
+        return carry
+
+    lax.fori_loop(0, positions, forward, 0)
+
+    def backward(p, carry):
+        for t in range(2):
+            for k in range(1, peers):
+                swap(p, t, k).wait_recv()
+
+            def scale(i, carry):
+                rows = pl.ds(pl.multiple_of(t * tile + i * step, step), step)
+                total = own[p, rows, :]
+                for k in range(peers - 1):
+                    total = total + other[k, p, rows, :]
+                ratio = amp_ref[p, rows, :].astype(f32) / jnp.sqrt(total + 1.0)
+                here = pl.ds(pl.multiple_of(i * step, step), step)
+
+                def fix(m, carry):
+                    for part in range(2):
+                        wave[p, m, t, part, here, :] = wave[p, m, t, part, here, :] * ratio
+                    return carry
+
+                lax.fori_loop(0, modes, fix, 0)
+                return carry
+
+            lax.fori_loop(0, tile // step, scale, 0)
+
+            def first(m, carry):
+                fixed = [wave[p, m, t, part].astype(bf16) for part in range(2)]
+                blocks = [fixed[part][:, col * tile : (col + 1) * tile] for col in range(2) for part in range(2)]
+                joined = jnp.concatenate(blocks, axis=1)
+                half = jnp.dot(joined, minus[...], preferred_element_type=f32).astype(bf16)
+                put(half, m, t)
+                return carry
+
+            lax.fori_loop(0, modes, first, 0)
+
+        def second(m, carry):
+            for t in range(2):
+                rows = pl.ds(t * tile, tile)
+                out = jnp.dot(plus[t * width : (t + 1) * width, :], stacked[m], preferred_element_type=f32)
+                for col in range(2):
+                    at = pl.ds(col * tile, tile)
+                    real, imag = out[:tile, col * tile : (col + 1) * tile], out[tile:, col * tile : (col + 1) * tile]
+                    obj_re = patch_ref[p, 0, rows, at].astype(f32)
+                    obj_im = patch_ref[p, 1, rows, at].astype(f32)
+                    diff_re = real - exits[p, m, rows, 2 * col * tile : (2 * col + 1) * tile].astype(f32)
+                    diff_im = imag - exits[p, m, rows, (2 * col + 1) * tile : (2 * col + 2) * tile].astype(f32)
+                    add_re = obj_re * diff_re + obj_im * diff_im
+                    add_im = obj_re * diff_im - obj_im * diff_re
+                    grad_ref[m, 0, rows, at] = jnp.where(p == 0, add_re, grad_ref[m, 0, rows, at] + add_re)
+                    grad_ref[m, 1, rows, at] = jnp.where(p == 0, add_im, grad_ref[m, 1, rows, at] + add_im)
+            return carry
+
+        lax.fori_loop(0, modes, second, 0)
+        return carry
+
+    lax.fori_loop(0, positions, backward, 0)
+    for p in range(positions):
+        for t in range(2):
+            for k in range(1, peers):
+                swap(p, t, k).wait_send()
+
+
+def front(base, probe, patches, amplitude):
     modes, width = probe.shape[1], probe.shape[2]
+    positions = patches.shape[0]
+    peers = lax.axis_size("mode")
+    tile = width // 2
+    dma = pltpu.SemaphoreType.DMA
+    f32, bf16 = jnp.float32, jnp.bfloat16
+    vmem = pl.BlockSpec(memory_space=pltpu.VMEM)
+    flops = positions * modes * 2 * 16 * width**3
     return pl.pallas_call(
-        forward_kernel,
-        grid=(modes,),
-        in_specs=[
-            whole(base.shape),
-            pl.BlockSpec((2, 1, width, width), lambda m: (0, m, 0, 0)),
-            whole(patch.shape),
+        functools.partial(front_kernel, peers),
+        in_specs=[vmem, pl.BlockSpec(memory_space=pl.ANY), vmem, vmem],
+        out_specs=vmem,
+        out_shape=jax.ShapeDtypeStruct((modes, 2, width, width), f32),
+        scratch_shapes=[
+            pltpu.VMEM((2 * width, 2 * width), bf16),
+            pltpu.VMEM((2 * width, 2 * width), bf16),
+            pltpu.VMEM((modes, 2, width, width), f32),
+            pltpu.VMEM((positions, modes, width, 2 * width), bf16),
+            pltpu.VMEM((positions, modes, 2, 2, tile, width), f32),
+            pltpu.VMEM((modes, 2 * width, width), bf16),
+            pltpu.VMEM((positions, width, width), f32),
+            pltpu.VMEM((max(peers - 1, 1), positions, width, width), f32),
+            dma((modes,)),
+            dma((max(peers - 1, 1), positions, 2)),
+            dma((max(peers - 1, 1), positions, 2)),
         ],
-        out_specs=[
-            pl.BlockSpec((1, 2, width, width), lambda m: (m, 0, 0, 0)),
-            pl.BlockSpec((1, 2, width, width), lambda m: (m, 0, 0, 0)),
-            whole((width, width)),
-        ],
-        out_shape=[
-            jax.ShapeDtypeStruct((modes, 2, width, width), jnp.float32),
-            jax.ShapeDtypeStruct((modes, 2, width, width), jnp.bfloat16),
-            jax.ShapeDtypeStruct((width, width), jnp.float32),
-        ],
-        scratch_shapes=table_scratch(width),
-        compiler_params=params(),
-        cost_estimate=cost(modes, width, modes * width * width * 20),
-        name="forward",
-    )(base, probe, patch)
-
-
-def backward(base, total, amplitude, index, wave, exits, patch, grad, start, count):
-    width = total.shape[0]
-    at = lambda m: (m + start, 0, 0, 0)
-    block = (1, 2, width, width)
-    operands = [base, total, amplitude, wave, exits, patch]
-    in_specs = [
-        whole(base.shape),
-        whole(total.shape),
-        pl.BlockSpec((1, width, width), lambda m: (index, 0, 0)),
-        pl.BlockSpec(block, at),
-        pl.BlockSpec(block, at),
-        whole(patch.shape),
-    ]
-    if grad is not None:
-        operands.append(grad)
-        in_specs.append(pl.BlockSpec(block, at))
-    return pl.pallas_call(
-        functools.partial(backward_kernel, grad is None),
-        grid=(count,),
-        in_specs=in_specs,
-        out_specs=pl.BlockSpec(block, lambda m: (m, 0, 0, 0)),
-        out_shape=jax.ShapeDtypeStruct((count, 2, width, width), jnp.float32),
-        scratch_shapes=table_scratch(width) + [pltpu.VMEM((width, width), jnp.float32)],
-        compiler_params=params(),
-        cost_estimate=cost(count, width, count * width * width * 24),
-        name="backward",
-    )(*operands)
+        compiler_params=pltpu.CompilerParams(collective_id=1, has_side_effects=True, vmem_limit_bytes=FRONT_LIMIT),
+        cost_estimate=pl.CostEstimate(flops=flops, bytes_accessed=0, transcendentals=0),
+        name="front",
+    )(base, probe, patches, amplitude)
 
 
 def split_lines(cores_total):
@@ -656,35 +660,23 @@
     )(prev_norm, sums, pre, probe, direction)
 
 
-def sum_over_modes(local_sum):
-    if lax.axis_size("mode") != 2:
-        return lax.psum(local_sum, "mode")
-    return local_sum + lax.ppermute(local_sum, "mode", [(0, 1), (1, 0)])
+def whole(shape):
+    return pl.BlockSpec(shape, lambda *_: (0,) * len(shape))
 
 
 def on_device(probe, prev_direction, prev_norm, object_tile, offsets, amplitude):
     width = probe.shape[2]
-    modes = probe.shape[1]
     positions = amplitude.shape[0]
-    base = base_table(width)
-    illum = jnp.zeros((width, width), jnp.float32)
-    patches, kept = [], []
-    for index in range(positions):
-        patch = lax.dynamic_slice(
-            object_tile, (jnp.int32(0), offsets[index, 0], offsets[index, 1]), (2, width, width)
-        )
-        patches.append(patch)
-        wave, exits, local_sum = forward(base, probe, patch)
-        total = sum_over_modes(local_sum)
-        kept.append((wave, exits, total))
-        wide = patch.astype(jnp.float32)
-        illum = illum + wide[0] * wide[0] + wide[1] * wide[1]
-    grad = None
-    for index in range(positions - 1):
-        wave, exits, total = kept[index]
-        grad = backward(base, total, amplitude, index, wave, exits, patches[index], grad, 0, modes)
-    wave, exits, total = kept[-1]
-    part = backward(base, total, amplitude, positions - 1, wave, exits, patches[-1], grad, 0, modes)
+    zero = jnp.int32(0)
+    patches = jnp.stack(
+        [
+            lax.dynamic_slice(object_tile, (zero, offsets[k, 0], offsets[k, 1]), (2, width, width))
+            for k in range(positions)
+        ]
+    )
+    wide = patches.astype(jnp.float32)
+    illum = jnp.sum(wide * wide, axis=(0, 1))
+    part = front(base_table(width), probe, patches, amplitude)
     pre, sums = reduce_grads(part, illum, prev_direction)
     return tuple(finish(prev_norm, sums, pre, probe, prev_direction))
 

time: 295 us -> 284 us (0.963)
  other arithmetic: 15.4 us -> 8.35 us
  waiting for transfers between devices: 3.99 us -> 0 us
  starting transfers between devices: 3.16 us -> 0 us
    add x3 -> x0, other arithmetic: 6.79 us -> none  [the longest x2 3.7 us: sum_over_modes(): return local_sum + lax.ppermute(local_sum, 'mode', [(0, 1), (1, 0)])]
    ppermute x2 -> x0, waiting for transfers between devices: 3.99 us -> none  [sum_over_modes(): return local_sum + lax.ppermute(local_sum, 'mode', [(0, 1), (1, 0)])]
    convert_element_type x1 -> x0, other arithmetic: 3.18 us -> none  [on_device(): wide = patch.astype(jnp.float32)]
    ppermute x2 -> x0, starting transfers between devices: 3.16 us -> none  [sum_over_modes(): return local_sum + lax.ppermute(local_sum, 'mode', [(0, 1), (1, 0)])]
    pallas_call x4 -> x1, Pallas kernels: 73.6 us -> 75.4 us  [front(): pl.pallas_call(functools.partial(front_kernel, peers), in_specs=[vmem, pl...]
    unnamed x14 -> x10, local copies, waits for them, and re-layouts: 7.48 us -> 7.47 us
  transfers between devices with their start and end apart: 2 -> 0, of which waited for: 2 -> 0; matrix products, arithmetic and copies ran while one was open for 2% -> 0% of each run, Pallas kernels for 12% -> 0%
where the time goes in v2:
time: 284 us; the launch traced here: 283 us
  Pallas kernels  256 us (90%)
  local copies, waits for them, and re-layouts  10.2 us (4%)
  between operations  8.59 us (3%)
  other arithmetic  8.35 us (3%)
    pallas_call x1, Pallas kernels, reduce_grads(): pl.pallas_call(functools.partial(reduce_kernel, shape, modes, width), in_...  165 us
    pallas_call x1, Pallas kernels, front(): pl.pallas_call(functools.partial(front_kernel, peers), in_specs=[vmem, pl...  75.4 us
    pallas_call x1, Pallas kernels, finish(): pl.pallas_call(finish_kernel, grid=(modes, width // rows), in_specs=[smem...  15.5 us
    unnamed x10, local copies, waits for them, and re-layouts  7.47 us

profile of v2, /device:TPU:0, one launch (start us, length us, event | category | flops | bytes accessed | tf_op | source)
XLA Modules:
  0.0 283.3 jit_solution(10718510653338791831)
XLA Ops:
  0.6 0.0 copy-start.4
  0.6 1.4 fusion.6
  10.0 4.4 %multiply_convert_fusion = (bf16[1,512,512]{2,1,0:T(8,128)(2,1)S(1)}, bf16[1,512,512]{2,1,0:T(8,128)(2,1)S(1)}) fusion(), kind=kLoop, calls=%fused_computation.11 | loop fusion | flops 4718592 | bytes 1048576 | tf_op jit(solution)/shard_map/convert_element_type | solution.py:22
  14.4 1.1 pad_maximum_fusion.1.base_ref
  15.4 0.0 copy-done.4
  15.4 1.3 dynamic-slice_bitcast_fusion.1
  16.7 1.4 multiply_reduce_fusion
  18.1 1.5 pad_maximum_fusion.patch_ref
  19.6 75.4 %front.1.grad_ref = f32[4,2,512,512]{3,2,1,0:T(8,128)} custom-call(bf16[2,512,512]{2,1,0:T(8,128)(2,1)} %pad_maximum_fusion.1.base_ref, f32[2,4,512,512]{3,2,1,0:T(8,128)} %probe_ref.3, bf16[2,2,512,512]{3,2,1,0:T(8,128)(2,1)} %pad_maximum_fusion.patch_ref, bf16[2,512,512]{2,1,0:T(8,128)(2,1)} %amp_ref.1), custom_call_target="tpu_custom_call" | custom-call | flops 34359738368 | tf_op jit(solution)/shard_map/front/pallas_call | solution.py:319
  95.0 0.0 copy-start.3
  95.0 165.3 %reduce.1 = (f32[4,2,512,512]{3,2,1,0:T(8,128)}, f32[24,128]{1,0:T(8,128)}) custom-call(f32[4,2,512,512]{3,2,1,0:T(8,128)} %front.1.grad_ref, f32[1,512,512]{2,1,0:T(8,128)} %bitcast.9, f32[2,4,512,512]{3,2,1,0:T(8,128)} %dir_ref.3), custom_call_target="tpu_custom_call" | custom-call | tf_op jit(solution)/shard_map/reduce/pallas_call | solution.py:601
  260.4 0.0 copy-done.3
  260.4 0.0 copy-start
  260.4 3.4 %copy-done = f32[2,4,512,512]{3,2,1,0:T(8,128)S(1)} copy-done((f32[2,4,512,512]{3,2,1,0:T(8,128)S(1)}, f32[2,4,512,512]{3,2,1,0:T(8,128)}, u32[]{:S(2)}) %copy-start) | copy-done | bytes 8388632
  263.8 0.0 copy-start.1
  263.8 3.4 %copy-done.1 = f32[4,2,512,512]{3,2,1,0:T(8,128)S(1)} copy-done((f32[4,2,512,512]{3,2,1,0:T(8,128)S(1)}, f32[4,2,512,512]{3,2,1,0:T(8,128)}, u32[]{:S(2)}) %copy-start.1) | copy-done | bytes 8388632
  267.1 0.0 copy-start.2
  267.1 0.7 copy-done.2
  267.8 15.5 %finish.1 = (f32[2,4,512,512]{3,2,1,0:T(8,128)}, f32[2,4,512,512]{3,2,1,0:T(8,128)}, f32[4]{0:T(128)}) custom-call(f32[4]{0:T(128)S(1)} %copy-done.3, f32[24,128]{1,0:T(8,128)S(1)} %copy-done.2, f32[4,2,512,512]{3,2,1,0:T(8,128)S(1)} %copy-done.1, f32[2,4,512,512]{3,2,1,0:T(8,128)S(1)} %copy-done, f32[2,4,512,512]{3,2,1,0:T(8,128)} %dir_ref.3), custom_call_target="tpu_custom_call" | custom-call | tf_op jit(solution)/shard_map/finish/pallas_call | solution.py:640
Async XLA Ops:
  0.6 14.8 %copy-start.4 = (bf16[2,640,640]{2,1,0:T(8,128)(2,1)S(1)}, bf16[2,640,640]{2,1,0:T(8,128)(2,1)}, u32[]{:S(2)}) copy-start(bf16[2,640,640]{2,1,0:T(8,128)(2,1)} %param.9) | copy-start | bytes 4915204
  95.0 165.3 %copy-start.3 = (f32[4]{0:T(128)S(1)}, f32[4]{0:T(128)}, u32[]{:S(2)}) copy-start(f32[4]{0:T(128)} %norm_ref.1) | copy-start | bytes 52
  260.4 3.4 %copy-start = (f32[2,4,512,512]{3,2,1,0:T(8,128)S(1)}, f32[2,4,512,512]{3,2,1,0:T(8,128)}, u32[]{:S(2)}) copy-start(f32[2,4,512,512]{3,2,1,0:T(8,128)} %probe_ref.3) | copy-start | bytes 25165828
  263.8 3.4 %copy-start.1 = (f32[4,2,512,512]{3,2,1,0:T(8,128)S(1)}, f32[4,2,512,512]{3,2,1,0:T(8,128)}, u32[]{:S(2)}) copy-start(f32[4,2,512,512]{3,2,1,0:T(8,128)} %get-tuple-element.6.pre_ref) | copy-start | bytes 25165828
  267.1 0.7 copy-start.2

commit v3 on v2

--- a/solution.py
+++ b/solution.py
@@ -11,6 +11,22 @@
 MESH = pl.DeviceIdType.MESH
 VMEM_LIMIT = 60 * 1024 * 1024
 FRONT_LIMIT = 67043328
+REDUCE_LIMIT = 33 * 1024 * 1024
+FINISH_LIMIT = 18 * 1024 * 1024
+ORDERS = {
+    (4, 2, 2, 4): (
+        (
+            0, 1, 0, 0, 2, 0, 0, 3, 2, 1, 0, 1, 1, 2, 1, 0, 0, 1, 2, 1, 3, 0, 0, 1, 3, 1, 0, 0, 3,
+            1, 3, 0, 1, 2, 3, 2, 0, 3, 2, 1, 3, 2, 3, 3, 2, 2, 0, 3, 3, 1, 1, 1, 3, 2, 2, 3, 2, 2,
+            3, 2,
+        ),
+        (
+            0, 1, 0, 0, 1, 0, 0, 0, 2, 1, 2, 1, 0, 3, 1, 0, 1, 1, 3, 0, 3, 1, 3, 2, 0, 3, 1, 3, 2,
+            0, 3, 0, 2, 1, 1, 2, 3, 2, 1, 3, 2, 0, 2, 1, 2, 3, 0, 0, 2, 1, 2, 3, 1, 2, 2, 3, 3, 2,
+            3, 3,
+        ),
+    ),
+}
 
 
 def base_table(width):
@@ -83,6 +99,9 @@
 
                 push(right, 1, right + 1)
 
+            if size > 2:
+                yield
+
             @pl.when(u > left)
             def _():
                 @pl.when(u < size - 1)
@@ -127,6 +146,9 @@
                 @pl.when(u < size - 1)
                 def _():
                     push(low, 0, 1)
+
+            if size > 2 and step > 0:
+                yield
 
             @pl.when(high < size)
             def _():
@@ -165,9 +187,12 @@
 
 
 def front_kernel(
-    peers, base_ref, probe_ref, patch_ref, amp_ref, grad_ref,
+    peers, shape, base_ref, probe_ref, patch_ref, amp_ref, grad_ref, light_ref, total_ref,
     plus, minus, probe, exits, wave, stacked, own, other, load_sem, send_sem, recv_sem,
+    lit, held, tile_in, tile_all, *rest,
 ):
+    slots, sc_s, sc_r, (core_s, core_r, bc_s, bc_r) = rest[0:4], rest[4:8], rest[8:12], rest[12:]
+    spot = Spot(*shape)
     positions, modes = exits.shape[0], exits.shape[1]
     width = base_ref.shape[1]
     tile = width // 2
@@ -178,6 +203,9 @@
     barrier = pltpu.get_barrier_semaphore()
     for k in range(1, peers):
         pl.semaphore_signal(barrier, inc=1, device_id={"mode": lax.rem(y + k, peers)}, device_id_type=MESH)
+    for k in range(1, spot.count):
+        to = lax.rem(spot.me + k, spot.count)
+        pl.semaphore_signal(barrier, inc=1, device_id={"grp": to}, device_id_type=MESH)
 
     def load(m):
         return pltpu.make_async_copy(probe_ref.at[:, m], probe.at[m], load_sem.at[m])
@@ -185,8 +213,8 @@
     for m in range(modes):
         load(m).start()
     build_tables(base_ref, plus, minus)
-    if peers > 1:
-        pl.semaphore_wait(barrier, peers - 1)
+    share = Shares(spot, width)
+    pl.semaphore_wait(barrier, peers - 1 + spot.count - 1)
 
     def swap(p, t, k):
         rows = pl.ds(t * tile, tile)
@@ -246,6 +274,44 @@
         return carry
 
     lax.fori_loop(0, positions, forward, 0)
+
+    def give():
+        away = rows_at(lit, (1 - spot.core) * share.part, share.part)
+        return remote(away, held, core_s.at[0], core_r.at[0], spot.partner())
+
+    def shine(i, carry):
+        rows = pl.ds(pl.multiple_of(i * step, step), step)
+        acc = jnp.zeros((step, width), f32)
+        for p in range(positions):
+            obj_re, obj_im = patch_ref[p, 0, rows, :].astype(f32), patch_ref[p, 1, rows, :].astype(f32)
+            acc = acc + obj_re * obj_re + obj_im * obj_im
+        lit[0, rows, :] = acc
+        return carry
+
+    def parts(path):
+        sems = [(slots[k], sc_s[k], sc_r[k]) for k in (2 * path, 2 * path + 1)]
+        return share.scatter_parts(path, held, sems)
+
+    def scatter(path):
+        for line, chunk, slot, send, recv in parts(path):
+            for _ in line.scatter(chunk, slot, send, recv):
+                pass
+        block = held[0, pl.ds(pl.multiple_of(share.offset[path], 8), share.own), :]
+        light_ref[0] = block
+        tile_in[...] = fold_lanes(block)
+
+    def scatter_end(path):
+        for line, chunk, slot, send, recv in parts(path):
+            line.scatter_end(chunk, slot, send, recv)
+
+    lax.fori_loop(0, width // step, shine, 0)
+    give().start()
+    give().wait_recv()
+    add_rows(held, lit, share.base, share.part)
+    per_path(spot, shape[2], scatter)
+    for copy in broadcast(spot, tile_in, tile_all, bc_s, bc_r):
+        copy.start()
+    tile_all[0] = tile_in[...]
 
     def backward(p, carry):
         for t in range(2):
@@ -301,6 +367,11 @@
         return carry
 
     lax.fori_loop(0, positions, backward, 0)
+    for copy in broadcast(spot, tile_in, tile_all, bc_s, bc_r):
+        copy.wait()
+    total_ref[...] = jnp.sum(tile_all[...], axis=0)
+    give().wait_send()
+    per_path(spot, shape[2], scatter_end)
     for p in range(positions):
         for t in range(2):
             for k in range(1, peers):
@@ -315,12 +386,19 @@
     dma = pltpu.SemaphoreType.DMA
     f32, bf16 = jnp.float32, jnp.bfloat16
     vmem = pl.BlockSpec(memory_space=pltpu.VMEM)
+    shape = split_lines(lax.axis_size("grp"))
+    sizes = scatter_sizes(shape, width)
+    count, lanes = lax.axis_size("grp"), min(128, width)
     flops = positions * modes * 2 * 16 * width**3
     return pl.pallas_call(
-        functools.partial(front_kernel, peers),
+        functools.partial(front_kernel, peers, shape),
         in_specs=[vmem, pl.BlockSpec(memory_space=pl.ANY), vmem, vmem],
-        out_specs=vmem,
-        out_shape=jax.ShapeDtypeStruct((modes, 2, width, width), f32),
+        out_specs=[vmem, vmem, vmem],
+        out_shape=[
+            jax.ShapeDtypeStruct((modes, 2, width, width), f32),
+            jax.ShapeDtypeStruct((1, sizes[1][1], width), f32),
+            jax.ShapeDtypeStruct((8, lanes), f32),
+        ],
         scratch_shapes=[
             pltpu.VMEM((2 * width, 2 * width), bf16),
             pltpu.VMEM((2 * width, 2 * width), bf16),
@@ -333,6 +411,17 @@
             dma((modes,)),
             dma((max(peers - 1, 1), positions, 2)),
             dma((max(peers - 1, 1), positions, 2)),
+            pltpu.VMEM((1, width, width), f32),
+            pltpu.VMEM((1, width // shape[2], width), f32),
+            pltpu.VMEM((8, lanes), f32),
+            pltpu.VMEM((count, 8, lanes), f32),
+            *[pltpu.VMEM((n + 1, 1, rows, width), f32) for n, rows in sizes],
+            *[dma((n,)) for n, _ in sizes],
+            *[dma((n + 1,)) for n, _ in sizes],
+            dma((1,)),
+            dma((1,)),
+            dma((count,)),
+            dma((count,)),
         ],
         compiler_params=pltpu.CompilerParams(collective_id=1, has_side_effects=True, vmem_limit_bytes=FRONT_LIMIT),
         cost_estimate=pl.CostEstimate(flops=flops, bytes_accessed=0, transcendentals=0),
@@ -340,13 +429,12 @@
     )(base, probe, patches, amplitude)
 
 
-def split_lines(cores_total):
-    cores = 2 if cores_total % 2 == 0 else 1
-    chips = cores_total // cores
+def split_lines(count):
+    cores = 2 if count % 2 == 0 else 1
+    chips = count // cores
     inner = 1
-    while inner * inner * 2 <= chips and chips % (inner * 2) == 0:
+    while inner * inner * 4 <= chips and chips % (inner * 2) == 0:
         inner *= 2
-    inner = inner if inner * inner <= chips else inner // 2
     return chips // inner, inner, cores
 
 
@@ -354,153 +442,130 @@
     def __init__(self, spot, width):
         outer, inner, cores = spot.sizes
         self.part = width // cores
-        self.half = self.part // 2
-        self.own = self.half // (outer * inner)
-        self.base = (spot.core * self.part, spot.core * self.part + self.half)
-        a_big, b_big = self.half // inner, self.half // outer
-        self.big = (a_big, b_big)
-        self.first = ("inner", "outer")
-        place = {"inner": spot.inner, "outer": spot.outer}
-        size = {"inner": inner, "outer": outer}
-        self.lines = tuple(Line(spot, name, size[name], place[name]) for name in ("inner", "outer"))
-        self.offset = (
-            spot.inner * a_big + spot.outer * self.own,
-            spot.outer * b_big + spot.inner * self.own,
-        )
-        self.group = (spot.inner * a_big, spot.outer * b_big)
-
-    def order(self, path):
-        return (self.lines[0], self.lines[1]) if path == 0 else (self.lines[1], self.lines[0])
+        self.own = self.part // (outer * inner)
+        self.base = spot.core * self.part
+        self.big = (self.part // inner, self.part // outer)
+        first = Line(spot, "inner", inner, spot.inner)
+        second = Line(spot, "outer", outer, spot.outer)
+        self.lines = ((first, second), (second, first))
+        self.group = (spot.inner * self.big[0], spot.outer * self.big[1])
+        self.offset = (self.group[0] + spot.outer * self.own, self.group[1] + spot.inner * self.own)
+
+    def scatter_parts(self, path, held, sems):
+        top = lambda k: rows_at(held, k * self.big[path], self.big[path])
+        low = lambda k: rows_at(held, self.group[path] + k * self.own, self.own)
+        return [(line, chunk) + pair for line, chunk, pair in zip(self.lines[path], (top, low), sems)]
+
+    def gather_parts(self, path, whole_ref, sems):
+        low = lambda k: rows_at(whole_ref, self.base + self.group[path] + k * self.own, self.own)
+        top = lambda k: rows_at(whole_ref, self.base + k * self.big[path], self.big[path])
+        return [(line, chunk) + pair for line, chunk, pair in zip(self.lines[path][::-1], (low, top), sems)]
 
 
 def rows_at(ref, start, count):
     return ref.at[:, pl.ds(pl.multiple_of(start, 8), count), :]
 
 
+def scatter_sizes(shape, width):
+    outer, inner, cores = shape
+    part = width // cores
+    own = part // (outer * inner)
+    return [(inner, part // inner), (outer, own), (outer, part // outer), (inner, own)]
+
+
+def add_rows(into, mine, start, count):
+    step = 32 if count % 32 == 0 else count
+
+    def add(i, carry):
+        rows = pl.ds(pl.multiple_of(i * step, 8), step)
+        into[:, rows, :] += mine[:, pl.ds(pl.multiple_of(start + i * step, 8), step), :]
+        return carry
+
+    lax.fori_loop(0, count // step, add, 0)
+
+
+def broadcast(spot, src, dst, send, recv):
+    copies = []
+    for step in range(1, spot.count):
+        to = lax.rem(spot.me + step, spot.count)
+        copies.append(remote(src, dst.at[step], send.at[step], recv.at[step], {"grp": to}))
+    return copies
+
+
+def per_path(spot, count, act):
+    for path in range(count):
+        @pl.when(spot.core == path)
+        def _():
+            act(path)
+
+
 def reduce_kernel(
-    shape, modes, width, grad_ref, illum_ref, dir_ref, pre_ref, sums_ref,
-    held, held_i, prev, shift_in, shift_all, sums_in, sums_all, *rest,
+    shape, modes, width, grad_ref, light_ref, total_ref, dir_ref, pre_ref, sums_ref,
+    held, prev, sums_in, sums_all, *rest,
 ):
     outer, inner, cores = shape
     spot = Spot(outer, inner, cores)
     share = Shares(spot, width)
-    (slots, islots, core_s, core_r, sc_s, sc_r, ga_s, ga_r, isc_s, isc_r, back_s, back_r, dir_sem, bc_s, bc_r) = (
-        rest[0:4], rest[4:8], *rest[8:10], rest[10:14], rest[14:18], rest[18:22], rest[22:26],
-        rest[26:30], rest[30:34], *rest[34:],
+    slots, (core_s, core_r), sc_s, sc_r, ga_s, ga_r, (back_s, back_r, dir_sem, bc_s, bc_r) = (
+        rest[0:4], rest[4:6], rest[6:10], rest[10:14], rest[14:18], rest[18:22], rest[22:]
     )
-    me, count = spot.me, spot.count
     pixels = float(width * width)
 
     barrier = pltpu.get_barrier_semaphore()
-    for step in range(1, count):
-        pl.semaphore_signal(barrier, inc=1, device_id={"grp": lax.rem(me + step, count)}, device_id_type=MESH)
-
-    loads = []
-    for path in range(2):
-        start = pl.multiple_of(share.base[path] + share.offset[path], 8)
+    for step in range(1, spot.count):
+        to = lax.rem(spot.me + step, spot.count)
+        pl.semaphore_signal(barrier, inc=1, device_id={"grp": to}, device_id_type=MESH)
+
+    def load(path, m):
+        start = pl.multiple_of(share.base + share.offset[path], 8)
+        return pltpu.make_async_copy(dir_ref.at[:, m, pl.ds(start, share.own), :], prev.at[m], dir_sem.at[m])
+
+    def fetch(path):
         for m in range(modes):
-            load = pltpu.make_async_copy(
-                dir_ref.at[:, m, pl.ds(start, share.own), :], prev.at[path, m], dir_sem.at[path, m]
-            )
-            load.start()
-            loads.append(load)
-    pl.semaphore_wait(barrier, count - 1)
-
-    def core_send(src, dst, item):
-        return remote(src, dst, core_s.at[item], core_r.at[item], spot.partner())
-
-    def partial(m):
-        return grad_ref.at[m] if m < modes else illum_ref
-
-    def keep(m):
-        return held.at[m] if m < modes else held_i
+            load(path, m).start()
+
+    per_path(spot, cores, fetch)
+    sums_in[...] = jnp.zeros_like(sums_in)
+    pl.semaphore_wait(barrier, spot.count - 1)
 
     def give(m):
         other = (1 - spot.core) * share.part
-        return core_send(rows_at(partial(m), other, share.part), keep(m), m)
-
-    items = [modes] + list(range(modes))
-    for m in items:
+        return remote(
+            rows_at(grad_ref.at[m], other, share.part), held.at[m], core_s.at[m], core_r.at[m], spot.partner()
+        )
+
+    for m in range(modes):
         give(m).start()
-
-    def pair(m, path):
-        if m < modes:
-            one, two = 2 * path, 2 * path + 1
-            return [(slots[k].at[m], sc_s[k].at[m], sc_r[k].at[m]) for k in (one, two)]
-        return [(islots[k], isc_s[k], isc_r[k]) for k in (2 * path, 2 * path + 1)]
+    shift = jnp.sum(total_ref[...]) / pixels
 
     def scatter_parts(m, path):
-        first, second = share.order(path)
-        at = path * share.half
-        top = lambda k: rows_at(keep(m), at + k * share.big[path], share.big[path])
-        low = lambda k: rows_at(keep(m), at + share.group[path] + k * share.own, share.own)
-        return [(line, chunk) + sems for line, chunk, sems in zip((first, second), (top, low), pair(m, path))]
+        sems = [(slots[k].at[m], sc_s[k].at[m], sc_r[k].at[m]) for k in (2 * path, 2 * path + 1)]
+        return share.scatter_parts(path, held.at[m], sems)
 
     def gather_parts(m, path):
-        second, first = share.order(path)
-        base = share.base[path]
-        low = lambda k: rows_at(pre_ref.at[m], base + share.group[path] + k * share.own, share.own)
-        top = lambda k: rows_at(pre_ref.at[m], base + k * share.big[path], share.big[path])
         sems = [(ga_s[k].at[m], ga_r[k].at[m]) for k in (2 * path, 2 * path + 1)]
-        return [(line, chunk) + pairs for line, chunk, pairs in zip((first, second), (low, top), sems)]
-
-    def home(m, path):
-        block = rows_at(pre_ref.at[m], share.base[path], share.half)
-        return remote(block, block, back_s.at[m, path], back_r.at[m, path], spot.partner())
-
-    def broadcast(src, dst, which):
-        copies = []
-        for step in range(1, count):
-            to = lax.rem(me + step, count)
-            copies.append(remote(src, dst.at[step], bc_s.at[which, step], bc_r.at[which, step], {"grp": to}))
-        return copies
-
-    def own_illum(path):
-        at = pl.multiple_of(path * share.half + share.offset[path], 8)
-        return held_i[0, pl.ds(at, share.own), :]
-
-    def scatter(m, path):
-        if path == 0:
-            give(m).wait_recv()
-            held_m, mine = keep(m), partial(m)
-            step = 32 if share.part % 32 == 0 else share.part
-
-            def add(i, carry):
-                rows = pl.ds(pl.multiple_of(i * step, 8), step)
-                held_m[:, rows, :] += mine[:, pl.ds(pl.multiple_of(spot.core * share.part + i * step, 8), step), :]
-                return carry
-
-            lax.fori_loop(0, share.part // step, add, 0)
+        return share.gather_parts(path, pre_ref.at[m], sems)
+
+    def home(m):
+        block = rows_at(pre_ref.at[m], share.base, share.part)
+        return remote(block, block, back_s.at[m], back_r.at[m], spot.partner())
+
+    def stream(m, path):
+        give(m).wait_recv()
+        add_rows(held.at[m], grad_ref.at[m], share.base, share.part)
         for line, chunk, slot, send, recv in scatter_parts(m, path):
             yield from line.scatter(chunk, slot, send, recv)
-
-    def illum_done():
-        tile = fold_lanes(own_illum(0)) + fold_lanes(own_illum(1))
-        shift_in[...] = tile
-        for copy in broadcast(shift_in, shift_all, 0):
-            copy.start()
-        shift_all[0] = tile
-
-    def shift_value():
-        for copy in broadcast(shift_in, shift_all, 0):
-            copy.wait_recv()
-        return jnp.sum(shift_all[...]) / pixels
-
-    def mode(m, path, shift):
-        yield from scatter(m, path)
-        at = pl.multiple_of(path * share.half + share.offset[path], 8)
-        rows = pl.ds(at, share.own)
-        to = pl.ds(pl.multiple_of(share.base[path] + share.offset[path], 8), share.own)
-        light = own_illum(path)
-        loads[path * modes + m].wait()
+        rows = pl.ds(pl.multiple_of(share.offset[path], 8), share.own)
+        to = pl.ds(pl.multiple_of(share.base + share.offset[path], 8), share.own)
+        light = light_ref[0]
+        load(path, m).wait()
         g_re, g_im = held[m, 0, rows, :], held[m, 1, rows, :]
-        d_re, d_im = prev[path, m, 0], prev[path, m, 1]
+        d_re, d_im = prev[m, 0], prev[m, 1]
         den = light + shift
         p_re, p_im = g_re / den, g_im / den
         pre_ref[m, 0, to, :] = p_re
         pre_ref[m, 1, to, :] = p_im
-        parts = gather_parts(m, path)
-        line, chunk, send, recv = parts[0]
+        (line, chunk, send, recv), later = gather_parts(m, path)
         walk = line.gather(chunk, send, recv)
         next(walk, None)
         terms = (
@@ -511,71 +576,67 @@
             light * (d_re * d_re + d_im * d_im),
         )
         for k, term in enumerate(terms):
-            tile = jnp.sum(fold_lanes(term), axis=0, keepdims=True)
             row = 5 * m + k
-            sums_in[row : row + 1, :] = tile if path == 0 else sums_in[row : row + 1, :] + tile
+            sums_in[row : row + 1, :] = jnp.sum(fold_lanes(term), axis=0, keepdims=True)
+        if m == modes - 1:
+            told.append(True)
         yield
         yield from walk
-        line, chunk, send, recv = parts[1]
+        line, chunk, send, recv = later
         yield from line.gather(chunk, send, recv)
-        home(m, path).start()
-
-    def run(streams):
-        streams = list(streams)
-        while streams:
-            alive = []
-            for stream in streams:
-                try:
-                    next(stream)
-                    alive.append(stream)
-                except StopIteration:
-                    pass
-            streams = alive
-
-    sums_in[...] = jnp.zeros_like(sums_in)
-    run([scatter(modes, 0), scatter(modes, 1)])
-    illum_done()
-    shift = shift_value()
-
-    def lagged(stream, lag):
-        for _ in range(lag):
-            yield
-        yield from stream
-
-    run(lagged(mode(m, path, shift), 2 * m) for m in range(modes) for path in range(2))
-
-    for copy in broadcast(sums_in, sums_all, 1):
-        copy.start()
-    sums_all[0] = sums_in[...]
-    for copy in broadcast(sums_in, sums_all, 1):
-        copy.wait_recv()
-    sums_ref[...] = jnp.sum(sums_all[...], axis=0)
-
-    for m in range(modes):
-        for path in range(2):
-            home(m, path).wait_recv()
-    for m in items:
-        give(m).wait_send()
-        for path in range(2):
+        home(m).start()
+
+    told = []
+
+    def share_sums():
+        for copy in broadcast(spot, sums_in, sums_all, bc_s, bc_r):
+            copy.start()
+
+    def run(path):
+        told.clear()
+        streams = [stream(m, path) for m in range(modes)]
+        done = set()
+        for m in turns(shape, modes, path):
+            if m in done:
+                continue
+            if next(streams[m], done) is done:
+                done.add(m)
+        share_sums()
+        sums_all[0] = sums_in[...]
+        for copy in broadcast(spot, sums_in, sums_all, bc_s, bc_r):
+            copy.wait_recv()
+        for m in range(modes):
+            home(m).wait_recv()
+        for m in range(modes):
+            give(m).wait_send()
             for line, chunk, slot, send, recv in scatter_parts(m, path):
                 line.scatter_end(chunk, slot, send, recv)
-            if m < modes:
-                for line, chunk, send, recv in gather_parts(m, path):
-                    line.gather_end(chunk, send, recv)
-                home(m, path).wait_send()
-    for which, src, dst in ((0, shift_in, shift_all), (1, sums_in, sums_all)):
-        for copy in broadcast(src, dst, which):
+            for line, chunk, send, recv in gather_parts(m, path):
+                line.gather_end(chunk, send, recv)
+            home(m).wait_send()
+        for copy in broadcast(spot, sums_in, sums_all, bc_s, bc_r):
             copy.wait_send()
 
-
-def reduce_grads(part, illum, direction):
+    per_path(spot, cores, run)
+    sums_ref[...] = jnp.sum(sums_all[...], axis=0)
+
+
+def turns(shape, modes, path):
+    key = (*shape, modes)
+    if key in ORDERS:
+        return ORDERS[key][path]
+    steps = 8 * (shape[0] + shape[1])
+    events = sorted((k + (3 * m) // 2, m) for m in range(modes) for k in range(steps))
+    return [m for _, m in events]
+
+
+def reduce_grads(part, light, total, direction):
     modes, _, width, _ = part.shape
     shape = split_lines(lax.axis_size("grp"))
     outer, inner, cores = shape
     count = outer * inner * cores
-    half = width // cores // 2
-    own = half // (outer * inner)
-    sizes = [(inner, half // inner), (outer, own), (outer, half // outer), (inner, own)]
+    sizes = scatter_sizes(shape, width)
+    own = sizes[1][1]
     back_sizes = [outer, inner, inner, outer]
     sum_rows = -(-5 * modes // 8) * 8
     lanes = min(128, width)
@@ -583,58 +644,68 @@
     f32 = jnp.float32
     scratch = [
         pltpu.VMEM((modes, 2, width // cores, width), f32),
-        pltpu.VMEM((1, width // cores, width), f32),
-        pltpu.VMEM((2, modes, 2, own, width), f32),
-        pltpu.VMEM((8, lanes), f32),
-        pltpu.VMEM((count, 8, lanes), f32),
+        pltpu.VMEM((modes, 2, own, width), f32),
         pltpu.VMEM((sum_rows, lanes), f32),
         pltpu.VMEM((count, sum_rows, lanes), f32),
     ]
     scratch += [pltpu.VMEM((modes, n + 1, 2, rows, width), f32) for n, rows in sizes]
-    scratch += [pltpu.VMEM((n + 1, 1, rows, width), f32) for n, rows in sizes]
-    scratch += [dma((modes + 1,)), dma((modes + 1,))]
+    scratch += [dma((modes,)), dma((modes,))]
     scratch += [dma((modes, n)) for n, _ in sizes] + [dma((modes, n + 1)) for n, _ in sizes]
     scratch += [dma((modes, 2, n)) for n in back_sizes] + [dma((modes, n)) for n in back_sizes]
-    scratch += [dma((n,)) for n, _ in sizes] + [dma((n + 1,)) for n, _ in sizes]
-    scratch += [dma((modes, 2)), dma((modes, 2)), dma((2, modes)), dma((2, count)), dma((2, count))]
+    scratch += [dma((modes,)), dma((modes,)), dma((modes,)), dma((count,)), dma((count,))]
     vmem = pl.BlockSpec(memory_space=pltpu.VMEM)
     return pl.pallas_call(
         functools.partial(reduce_kernel, shape, modes, width),
-        in_specs=[vmem, vmem, pl.BlockSpec(memory_space=pl.ANY)],
+        in_specs=[vmem, vmem, vmem, pl.BlockSpec(memory_space=pl.ANY)],
         out_specs=[vmem, vmem],
         out_shape=[
             jax.ShapeDtypeStruct(part.shape, f32),
             jax.ShapeDtypeStruct((sum_rows, lanes), f32),
         ],
         scratch_shapes=scratch,
-        compiler_params=pltpu.CompilerParams(collective_id=0, has_side_effects=True, vmem_limit_bytes=VMEM_LIMIT),
+        compiler_params=pltpu.CompilerParams(collective_id=0, has_side_effects=True, vmem_limit_bytes=REDUCE_LIMIT),
+        cost_estimate=pl.CostEstimate(flops=10**10, bytes_accessed=0, transcendentals=0),
         name="reduce",
-    )(part, illum[None], direction)
-
-
-def finish_kernel(norm_ref, sums_ref, pre_ref, probe_ref, dir_ref, new_probe, new_dir, new_norm):
+    )(part, light, total, direction)
+
+
+def finish_kernel(norm_ref, sums_ref, pre_ref, probe_ref, dir_ref, new_probe, new_dir, new_norm, kept):
     mode = pl.program_id(0)
     pixels = float(new_probe.shape[3] ** 2)
-    index = lax.broadcasted_iota(jnp.int32, sums_ref.shape, 0)
-
-    def mean(k):
-        return jnp.sum(jnp.where(index == 5 * mode + k, sums_ref[...], 0.0)) / pixels
-
-    norm, cross, light, light_cross, light_prev = (mean(k) for k in range(5))
-    new_norm[mode] = norm
-    beta = norm / norm_ref[mode]
-    upper = norm + beta * cross
-    lower = light + beta * (2.0 * light_cross + beta * light_prev)
-    alpha = upper / (lower + 1.0)
-    for part in range(2):
-        step = pre_ref[0, part] + beta * dir_ref[part, 0]
-        new_dir[part, 0] = step
-        new_probe[part, 0] = probe_ref[part, 0] + alpha * step
+
+    @pl.when(pl.program_id(1) == 0)
+    def _():
+        index = lax.broadcasted_iota(jnp.int32, sums_ref.shape, 0)
+
+        def mean(k):
+            return jnp.sum(jnp.where(index == 5 * mode + k, sums_ref[...], 0.0)) / pixels
+
+        norm, cross, light, light_cross, light_prev = (mean(k) for k in range(5))
+        new_norm[mode] = norm
+        beta = norm / norm_ref[mode]
+        upper = norm + beta * cross
+        lower = light + beta * (2.0 * light_cross + beta * light_prev)
+        kept[0] = beta
+        kept[1] = upper / (lower + 1.0)
+
+    beta, alpha = kept[0], kept[1]
+    rows = new_probe.shape[2]
+    small = min(32, rows)
+
+    def body(i, carry):
+        at = pl.ds(pl.multiple_of(i * small, small), small)
+        for part in range(2):
+            step = pre_ref[0, part, at, :] + beta * dir_ref[part, 0, at, :]
+            new_dir[part, 0, at, :] = step
+            new_probe[part, 0, at, :] = probe_ref[part, 0, at, :] + alpha * step
+        return carry
+
+    lax.fori_loop(0, rows // small, body, 0)
 
 
 def finish(prev_norm, sums, pre, probe, direction):
     modes, width = probe.shape[1], probe.shape[2]
-    rows = min(128, width)
+    rows = min(256, width)
     block = pl.BlockSpec((2, 1, rows, width), lambda m, r: (0, m, r, 0))
     smem = pl.BlockSpec(memory_space=pltpu.SMEM)
     return pl.pallas_call(
@@ -653,8 +724,9 @@
             jax.ShapeDtypeStruct(probe.shape, jnp.float32),
             jax.ShapeDtypeStruct((modes,), jnp.float32),
         ],
+        scratch_shapes=[pltpu.SMEM((2,), jnp.float32)],
         compiler_params=pltpu.CompilerParams(
-            dimension_semantics=("arbitrary", "arbitrary"), vmem_limit_bytes=32 * 1024 * 1024
+            dimension_semantics=("arbitrary", "arbitrary"), vmem_limit_bytes=FINISH_LIMIT
         ),
         name="finish",
     )(prev_norm, sums, pre, probe, direction)
@@ -674,10 +746,8 @@
             for k in range(positions)
         ]
     )
-    wide = patches.astype(jnp.float32)
-    illum = jnp.sum(wide * wide, axis=(0, 1))
-    part = front(base_table(width), probe, patches, amplitude)
-    pre, sums = reduce_grads(part, illum, prev_direction)
+    part, light, total = front(base_table(width), probe, patches, amplitude)
+    pre, sums = reduce_grads(part, light, total, prev_direction)
     return tuple(finish(prev_norm, sums, pre, probe, prev_direction))
 
 

time: 284 us -> 249 us (0.88)
  Pallas kernels: 256 us -> 217 us
  local copies, waits for them, and re-layouts: 10.2 us -> 16.1 us
    pallas_call x1, Pallas kernels: 165 us -> 122 us  [reduce_grads(): pl.pallas_call(functools.partial(reduce_kernel, shape, modes, width), in_...]
    pallas_call x1, Pallas kernels: 75.4 us -> 85.7 us  [front(): pl.pallas_call(functools.partial(front_kernel, peers, shape), in_specs=[v...]
    pallas_call x1, Pallas kernels: 15.5 us -> 8.79 us  [finish(): pl.pallas_call(finish_kernel, grid=(modes, width // rows), in_specs=[smem...]
    unnamed x10 -> x12, local copies, waits for them, and re-layouts: 7.47 us -> 11.7 us
where the time goes in v3:
time: 249 us; the launch traced here: 248 us
  Pallas kernels  217 us (87%)
  local copies, waits for them, and re-layouts  16.1 us (6%)
  between operations  8.41 us (3%)
  other arithmetic  6.96 us (3%)
    pallas_call x1, Pallas kernels, reduce_grads(): pl.pallas_call(functools.partial(reduce_kernel, shape, modes, width), in_...  122 us
    pallas_call x1, Pallas kernels, front(): pl.pallas_call(functools.partial(front_kernel, peers, shape), in_specs=[v...  85.7 us
    unnamed x12, local copies, waits for them, and re-layouts  11.7 us
    pallas_call x1, Pallas kernels, finish(): pl.pallas_call(finish_kernel, grid=(modes, width // rows), in_specs=[smem...  8.79 us

profile of v3, /device:TPU:0, one launch (start us, length us, event | category | flops | bytes accessed | tf_op | source)
XLA Modules:
  0.0 248.3 jit_solution(2278368188729755718)
XLA Ops:
  0.6 1.4 fusion.6
  9.8 4.4 %multiply_convert_fusion = (bf16[1,512,512]{2,1,0:T(8,128)(2,1)S(1)}, bf16[1,512,512]{2,1,0:T(8,128)(2,1)S(1)}) fusion(), kind=kLoop, calls=%fused_computation.10 | loop fusion | flops 4718592 | bytes 1048576 | tf_op jit(solution)/shard_map/convert_element_type | solution.py:38
  14.2 1.1 pad_maximum_fusion.1.base_ref
  15.2 3.0 %dynamic-slice_bitcast_fusion.1 = (bf16[1,2,512,512]{3,2,1,0:T(8,128)(2,1)S(1)}, bf16[1,2,512,512]{3,2,1,0:T(8,128)(2,1)S(1)}) fusion(bf16[2,640,640]{2,1,0:T(8,128)(2,1)} %param.9, s32[]{:T(128)S(6)} %select_n.33, s32[]{:T(128)S(6)} %select_n.34, s32[]{:T(128)S(6)} %select_n.35, s32[]{:T(128)S(6)} %select_n.36), kind=kLoop, calls=%fused_computation.9 | loop fusion | bytes 4194320 | tf_op jit(solution)/shard_map/stack | solution.py:743
  18.3 1.5 pad_maximum_fusion.patch_ref
  19.8 85.7 %front.1 = (f32[4,2,512,512]{3,2,1,0:T(8,128)}, f32[1,32,512]{2,1,0:T(8,128)}, f32[8,128]{1,0:T(8,128)}) custom-call(bf16[2,512,512]{2,1,0:T(8,128)(2,1)} %pad_maximum_fusion.1.base_ref, f32[2,4,512,512]{3,2,1,0:T(8,128)} %probe_ref.3, bf16[2,2,512,512]{3,2,1,0:T(8,128)(2,1)} %pad_maximum_fusion.patch_ref, bf16[2,512,512]{2,1,0:T(8,128)(2,1)} %amp_ref.1), custom_call_target="tpu_custom_call" | custom-call | flops 34359738368 | tf_op jit(solution)/shard_map/front/pallas_call | solution.py:393
  105.5 0.0 copy-start.3
  105.5 3.4 %copy-done.3 = f32[4,2,512,512]{3,2,1,0:T(8,128)S(1)} copy-done((f32[4,2,512,512]{3,2,1,0:T(8,128)S(1)}, f32[4,2,512,512]{3,2,1,0:T(8,128)}, u32[]{:S(2)}) %copy-start.3) | copy-done | bytes 8388632
  108.8 0.0 copy-start.4
  108.8 0.8 copy-done.4
  109.7 0.0 copy-start.5
  109.7 0.7 copy-done.5
  110.4 0.0 copy-start.2
  110.4 122.4 %reduce.1 = (f32[4,2,512,512]{3,2,1,0:T(8,128)S(1)}, f32[24,128]{1,0:T(8,128)S(1)}) custom-call(f32[4,2,512,512]{3,2,1,0:T(8,128)S(1)} %copy-done.3, f32[1,32,512]{2,1,0:T(8,128)S(1)} %copy-done.4, f32[8,128]{1,0:T(8,128)S(1)} %copy-done.5, f32[2,4,512,512]{3,2,1,0:T(8,128)} %dir_ref.3), custom_call_target="tpu_custom_call" | custom-call | flops 10000000000 | tf_op jit(solution)/shard_map/reduce/pallas_call | solution.py:657
  232.8 0.0 copy-done.2
  232.8 0.0 copy-start
  232.8 3.4 %copy-done = f32[2,4,512,512]{3,2,1,0:T(8,128)S(1)} copy-done((f32[2,4,512,512]{3,2,1,0:T(8,128)S(1)}, f32[2,4,512,512]{3,2,1,0:T(8,128)}, u32[]{:S(2)}) %copy-start) | copy-done | bytes 8388632
  236.2 0.0 copy-start.1
  236.2 3.4 %copy-done.1 = f32[2,4,512,512]{3,2,1,0:T(8,128)S(1)} copy-done((f32[2,4,512,512]{3,2,1,0:T(8,128)S(1)}, f32[2,4,512,512]{3,2,1,0:T(8,128)}, u32[]{:S(2)}) %copy-start.1) | copy-done | bytes 8388632
  239.6 8.8 %finish.1 = (f32[2,4,512,512]{3,2,1,0:T(8,128)}, f32[2,4,512,512]{3,2,1,0:T(8,128)}, f32[4]{0:T(128)}) custom-call(f32[4]{0:T(128)S(1)} %copy-done.2, f32[24,128]{1,0:T(8,128)S(1)} %get-tuple-element.11.sums_ref, f32[4,2,512,512]{3,2,1,0:T(8,128)S(1)} %get-tuple-element.12.pre_ref, f32[2,4,512,512]{3,2,1,0:T(8,128)S(1)} %copy-done, ...), custom_call_target="tpu_custom_call" | custom-call | tf_op jit(solution)/shard_map/finish/pallas_call | solution.py:711
Async XLA Ops:
  105.5 3.4 %copy-start.3 = (f32[4,2,512,512]{3,2,1,0:T(8,128)S(1)}, f32[4,2,512,512]{3,2,1,0:T(8,128)}, u32[]{:S(2)}) copy-start(f32[4,2,512,512]{3,2,1,0:T(8,128)} %get-tuple-element.8.grad_ref) | copy-start | bytes 25165828
  108.8 0.8 copy-start.4
  109.7 0.7 copy-start.5
  110.4 122.4 %copy-start.2 = (f32[4]{0:T(128)S(1)}, f32[4]{0:T(128)}, u32[]{:S(2)}) copy-start(f32[4]{0:T(128)} %norm_ref.1) | copy-start | bytes 52
  232.8 3.4 %copy-start = (f32[2,4,512,512]{3,2,1,0:T(8,128)S(1)}, f32[2,4,512,512]{3,2,1,0:T(8,128)}, u32[]{:S(2)}) copy-start(f32[2,4,512,512]{3,2,1,0:T(8,128)} %probe_ref.3) | copy-start | bytes 25165828
  236.2 3.4 %copy-start.1 = (f32[2,4,512,512]{3,2,1,0:T(8,128)S(1)}, f32[2,4,512,512]{3,2,1,0:T(8,128)}, u32[]{:S(2)}) copy-start(f32[2,4,512,512]{3,2,1,0:T(8,128)} %dir_ref.3) | copy-start | bytes 25165828

commit v4 on v3

--- a/solution.py
+++ b/solution.py
@@ -2,6 +2,7 @@
 import math
 
 import jax
+import numpy as np
 import jax.numpy as jnp
 from jax import lax
 from jax.experimental import pallas as pl
@@ -12,17 +13,18 @@
 VMEM_LIMIT = 60 * 1024 * 1024
 FRONT_LIMIT = 67043328
 REDUCE_LIMIT = 33 * 1024 * 1024
+CUT_LIMIT = 16 * 1024 * 1024
 FINISH_LIMIT = 18 * 1024 * 1024
 ORDERS = {
     (4, 2, 2, 4): (
         (
-            0, 1, 0, 0, 2, 0, 0, 3, 2, 1, 0, 1, 1, 2, 1, 0, 0, 1, 2, 1, 3, 0, 0, 1, 3, 1, 0, 0, 3,
-            1, 3, 0, 1, 2, 3, 2, 0, 3, 2, 1, 3, 2, 3, 3, 2, 2, 0, 3, 3, 1, 1, 1, 3, 2, 2, 3, 2, 2,
-            3, 2,
+            0, 1, 3, 0, 1, 0, 1, 1, 0, 2, 1, 0, 0, 0, 3, 1, 1, 2, 1, 0, 2, 3, 1, 1, 1, 3, 0, 0, 2,
+            2, 1, 2, 3, 1, 2, 0, 3, 2, 0, 0, 3, 3, 1, 0, 2, 2, 2, 1, 2, 2, 3, 3, 2, 3, 3, 3, 3, 0,
+            2, 3,
         ),
         (
-            0, 1, 0, 0, 1, 0, 0, 0, 2, 1, 2, 1, 0, 3, 1, 0, 1, 1, 3, 0, 3, 1, 3, 2, 0, 3, 1, 3, 2,
-            0, 3, 0, 2, 1, 1, 2, 3, 2, 1, 3, 2, 0, 2, 1, 2, 3, 0, 0, 2, 1, 2, 3, 1, 2, 2, 3, 3, 2,
+            0, 1, 0, 0, 1, 0, 3, 2, 0, 1, 0, 2, 0, 3, 1, 2, 1, 1, 0, 1, 0, 2, 2, 0, 1, 0, 3, 3, 3,
+            1, 2, 2, 0, 3, 0, 2, 0, 2, 1, 3, 2, 1, 3, 1, 2, 3, 2, 3, 1, 1, 1, 2, 2, 2, 3, 3, 0, 3,
             3, 3,
         ),
     ),
@@ -30,13 +32,12 @@
 
 
 def base_table(width):
-    index = jnp.arange(width, dtype=jnp.int32)
+    index = np.arange(width, dtype=np.int64)
     product = index[:, None] * index[None, :] % width
-    angle = -2.0 * math.pi / width * product.astype(jnp.float32)
-    scale = 1.0 / math.sqrt(width)
-    real_part = (jnp.cos(angle) * scale).astype(jnp.bfloat16)
-    imag_part = (jnp.sin(angle) * scale).astype(jnp.bfloat16)
-    return jnp.stack([real_part, imag_part])
+    angle = np.float32(-2.0 * math.pi / width) * product.astype(np.float32)
+    scale = np.float32(1.0 / math.sqrt(width))
+    both = np.stack([np.cos(angle) * scale, np.sin(angle) * scale])
+    return jnp.asarray(both.astype(jnp.bfloat16))
 
 
 def fold_lanes(block):
@@ -732,20 +733,58 @@
     )(prev_norm, sums, pre, probe, direction)
 
 
+def cut_kernel(offset_ref, tile_ref, patch_ref, wide):
+    positions, width, full = patch_ref.shape[0], patch_ref.shape[2], tile_ref.shape[2]
+    step = 64 if width % 64 == 0 else width
+
+    def widen(i, carry):
+        rows = pl.ds(pl.multiple_of(i * step, step), step)
+        for part in range(2):
+            wide[part, rows, :] = tile_ref[part, rows, :].astype(jnp.float32)
+        return carry
+
+    lax.fori_loop(0, full // step, widen, 0)
+
+    def position(p, carry):
+        row, col = offset_ref[p, 0], offset_ref[p, 1]
+        turn = lax.rem(full - col, full)
+        low = lax.rem(row, 8)
+        lift = lax.rem(step + 8 - low, step + 8)
+
+        def body(i, carry):
+            for part in range(2):
+                block = wide[part, pl.ds(pl.multiple_of(row - low + i * step, 8), step + 8), :]
+                block = pltpu.roll(pltpu.roll(block, lift, 0)[:step], turn, 1)[:, :width]
+                patch_ref[p, part, pl.ds(pl.multiple_of(i * step, step), step), :] = block.astype(jnp.bfloat16)
+            return carry
+
+        lax.fori_loop(0, width // step, body, 0)
+        return carry
+
+    lax.fori_loop(0, positions, position, 0)
+
+
+def cut(offsets, tile, width):
+    positions = offsets.shape[0]
+    vmem = pl.BlockSpec(memory_space=pltpu.VMEM)
+    return pl.pallas_call(
+        cut_kernel,
+        in_specs=[pl.BlockSpec(memory_space=pltpu.SMEM), vmem],
+        out_specs=vmem,
+        out_shape=jax.ShapeDtypeStruct((positions, 2, width, width), jnp.bfloat16),
+        scratch_shapes=[pltpu.VMEM((2, tile.shape[1] + 8, tile.shape[2]), jnp.float32)],
+        compiler_params=pltpu.CompilerParams(vmem_limit_bytes=CUT_LIMIT),
+        name="cut",
+    )(offsets, tile)
+
+
 def whole(shape):
     return pl.BlockSpec(shape, lambda *_: (0,) * len(shape))
 
 
 def on_device(probe, prev_direction, prev_norm, object_tile, offsets, amplitude):
     width = probe.shape[2]
-    positions = amplitude.shape[0]
-    zero = jnp.int32(0)
-    patches = jnp.stack(
-        [
-            lax.dynamic_slice(object_tile, (zero, offsets[k, 0], offsets[k, 1]), (2, width, width))
-            for k in range(positions)
-        ]
-    )
+    patches = cut(offsets, object_tile, width)
     part, light, total = front(base_table(width), probe, patches, amplitude)
     pre, sums = reduce_grads(part, light, total, prev_direction)
     return tuple(finish(prev_norm, sums, pre, probe, prev_direction))

time: 249 us -> 234 us (0.940)
  between operations: 8.41 us -> 0.69 us
  other arithmetic: 6.96 us -> 0 us
    unnamed x12 -> x22, local copies, waits for them, and re-layouts: 11.7 us -> 18.5 us
    pallas_call x1, Pallas kernels: 122 us -> 117 us  [reduce_grads(): pl.pallas_call(functools.partial(reduce_kernel, shape, modes, width), in_...]
    convert_element_type x1 -> x0, other arithmetic: 4.39 us -> none  [base_table(): imag_part = (jnp.sin(angle) * scale).astype(jnp.bfloat16)]
    pallas_call x0 -> x1, Pallas kernels: none -> 3.53 us  [cut(): pl.pallas_call(cut_kernel, in_specs=[pl.BlockSpec(memory_space=pltpu.SMEM...]
    another operation x1 -> x0, local copies, waits for them, and re-layouts: 3.03 us -> none  [on_device(): jnp.stack([lax.dynamic_slice(object_tile, (zero, offsets[k, 0], offsets[k...]
    another operation x2 -> x0, other arithmetic: 2.56 us -> none  [the longest x1 1.5 us: on_device(): jnp.stack([lax.dynamic_slice(object_tile, (zero, offsets[k, 0], offsets[k...]
where the time goes in v4:
time: 234 us
  Pallas kernels  215 us (92%)
  local copies, waits for them, and re-layouts  18.5 us (8%)
    pallas_call x1, Pallas kernels, reduce_grads(): pl.pallas_call(functools.partial(reduce_kernel, shape, modes, width), in_...  117 us
    pallas_call x1, Pallas kernels, front(): pl.pallas_call(functools.partial(front_kernel, peers, shape), in_specs=[v...  85.7 us
    unnamed x22, local copies, waits for them, and re-layouts  18.5 us
    pallas_call x1, Pallas kernels, finish(): pl.pallas_call(finish_kernel, grid=(modes, width // rows), in_specs=[smem...  8.79 us

profile of v4, /device:TPU:0, one launch (start us, length us, event | category | flops | bytes accessed | tf_op | source)
XLA Modules:
  0.0 233.9 jit_solution(315372913638993798)
XLA Ops:
  0.6 0.0 copy-start.5
  0.6 1.4 copy-done.5
  2.1 0.0 copy-start.6
  2.1 0.7 copy-done.6
  2.7 3.5 %cut.1.patch_ref = bf16[2,2,512,512]{3,2,1,0:T(8,128)(2,1)S(1)} custom-call(s32[2,2]{1,0:T(2,128)S(1)} %copy-done.6, bf16[2,640,640]{2,1,0:T(8,128)(2,1)S(1)} %copy-done.5), custom_call_target="tpu_custom_call" | custom-call | tf_op jit(solution)/shard_map/cut/pallas_call | solution.py:770
  6.3 0.0 copy-start.4
  6.3 1.3 copy-done.4
  7.6 85.7 %front.1 = (f32[4,2,512,512]{3,2,1,0:T(8,128)}, f32[1,32,512]{2,1,0:T(8,128)}, f32[8,128]{1,0:T(8,128)}) custom-call(bf16[2,512,512]{2,1,0:T(8,128)(2,1)} %constant.2.clone.base_ref, f32[2,4,512,512]{3,2,1,0:T(8,128)} %probe_ref.3, bf16[2,2,512,512]{3,2,1,0:T(8,128)(2,1)} %copy-done.4, bf16[2,512,512]{2,1,0:T(8,128)(2,1)} %amp_ref.1), custom_call_target="tpu_custom_call" | custom-call | flops 34359738368 | tf_op jit(solution)/shard_map/front/pallas_call | solution.py:394
  93.4 0.0 copy-start.8
  93.4 3.4 %copy-done.8 = f32[4,2,512,512]{3,2,1,0:T(8,128)S(1)} copy-done((f32[4,2,512,512]{3,2,1,0:T(8,128)S(1)}, f32[4,2,512,512]{3,2,1,0:T(8,128)}, u32[]{:S(2)}) %copy-start.8) | copy-done | bytes 8388632
  96.7 0.0 copy-start.9
  96.7 0.8 copy-done.9
  97.6 0.0 copy-start.10
  97.6 0.7 copy-done.10
  98.3 0.0 copy-start
  98.3 0.0 copy-start.7
  98.3 116.7 %reduce.1 = (f32[4,2,512,512]{3,2,1,0:T(8,128)S(1)}, f32[24,128]{1,0:T(8,128)S(1)}) custom-call(f32[4,2,512,512]{3,2,1,0:T(8,128)S(1)} %copy-done.8, f32[1,32,512]{2,1,0:T(8,128)S(1)} %copy-done.9, f32[8,128]{1,0:T(8,128)S(1)} %copy-done.10, f32[2,4,512,512]{3,2,1,0:T(8,128)} %dir_ref.3), custom_call_target="tpu_custom_call" | custom-call | flops 10000000000 | tf_op jit(solution)/shard_map/reduce/pallas_call | solution.py:658
  215.0 0.0 copy-start.2
  215.0 3.4 %copy-done.2 = f32[4,2,512,512]{3,2,1,0:T(8,128)} copy-done((f32[4,2,512,512]{3,2,1,0:T(8,128)}, f32[4,2,512,512]{3,2,1,0:T(8,128)S(1)}, u32[]{:S(2)}) %copy-start.2) | copy-done | bytes 8388632
  218.4 0.0 copy-done
  218.4 0.0 copy-done.7
  218.4 0.0 copy-start.1
  218.4 3.4 %copy-done.1 = f32[2,4,512,512]{3,2,1,0:T(8,128)S(1)} copy-done((f32[2,4,512,512]{3,2,1,0:T(8,128)S(1)}, f32[2,4,512,512]{3,2,1,0:T(8,128)}, u32[]{:S(2)}) %copy-start.1) | copy-done | bytes 8388632
  221.8 0.0 copy-start.3
  221.8 3.4 %copy-done.3 = f32[4,2,512,512]{3,2,1,0:T(8,128)S(1)} copy-done((f32[4,2,512,512]{3,2,1,0:T(8,128)S(1)}, f32[4,2,512,512]{3,2,1,0:T(8,128)}, u32[]{:S(2)}) %copy-start.3) | copy-done | bytes 8388632
  225.1 8.8 %finish.1 = (f32[2,4,512,512]{3,2,1,0:T(8,128)}, f32[2,4,512,512]{3,2,1,0:T(8,128)}, f32[4]{0:T(128)}) custom-call(f32[4]{0:T(128)S(1)} %copy-done.7, f32[24,128]{1,0:T(8,128)S(1)} %get-tuple-element.11.sums_ref, f32[4,2,512,512]{3,2,1,0:T(8,128)S(1)} %copy-done.3, f32[2,4,512,512]{3,2,1,0:T(8,128)S(1)} %copy-done, f32[2,4,512,512]{3,2,1,0:T(8,128)S(1)} %copy-done.1), custom_call_target="tpu_custom_call" | custom-call | tf_op jit(solution)/shard_map/finish/pallas_call | solution.py:712
Async XLA Ops:
  0.6 1.4 copy-start.5
  2.1 0.7 copy-start.6
  6.3 1.3 copy-start.4
  93.4 3.4 %copy-start.8 = (f32[4,2,512,512]{3,2,1,0:T(8,128)S(1)}, f32[4,2,512,512]{3,2,1,0:T(8,128)}, u32[]{:S(2)}) copy-start(f32[4,2,512,512]{3,2,1,0:T(8,128)} %get-tuple-element.8.grad_ref) | copy-start | bytes 25165828
  96.7 0.8 copy-start.9
  97.6 0.7 copy-start.10
  98.3 120.1 %copy-start = (f32[2,4,512,512]{3,2,1,0:T(8,128)S(1)}, f32[2,4,512,512]{3,2,1,0:T(8,128)}, u32[]{:S(2)}) copy-start(f32[2,4,512,512]{3,2,1,0:T(8,128)} %probe_ref.3) | copy-start | bytes 25165828
  98.3 120.1 %copy-start.7 = (f32[4]{0:T(128)S(1)}, f32[4]{0:T(128)}, u32[]{:S(2)}) copy-start(f32[4]{0:T(128)} %norm_ref.1) | copy-start | bytes 52
  215.0 3.4 %copy-start.2 = (f32[4,2,512,512]{3,2,1,0:T(8,128)}, f32[4,2,512,512]{3,2,1,0:T(8,128)S(1)}, u32[]{:S(2)}) copy-start(f32[4,2,512,512]{3,2,1,0:T(8,128)S(1)} %get-tuple-element.12.pre_ref) | copy-start | bytes 25165828
  218.4 3.4 %copy-start.1 = (f32[2,4,512,512]{3,2,1,0:T(8,128)S(1)}, f32[2,4,512,512]{3,2,1,0:T(8,128)}, u32[]{:S(2)}) copy-start(f32[2,4,512,512]{3,2,1,0:T(8,128)} %dir_ref.3) | copy-start | bytes 25165828
  221.8 3.4 %copy-start.3 = (f32[4,2,512,512]{3,2,1,0:T(8,128)S(1)}, f32[4,2,512,512]{3,2,1,0:T(8,128)}, u32[]{:S(2)}) copy-start(f32[4,2,512,512]{3,2,1,0:T(8,128)} %copy-done.2) | copy-start | bytes 25165828

commit v5 on v4

--- a/solution.py
+++ b/solution.py
@@ -12,20 +12,19 @@
 MESH = pl.DeviceIdType.MESH
 VMEM_LIMIT = 60 * 1024 * 1024
 FRONT_LIMIT = 67043328
-REDUCE_LIMIT = 33 * 1024 * 1024
 CUT_LIMIT = 16 * 1024 * 1024
-FINISH_LIMIT = 18 * 1024 * 1024
+FINISH_LIMIT = 60 * 1024 * 1024
 ORDERS = {
     (4, 2, 2, 4): (
         (
-            0, 1, 3, 0, 1, 0, 1, 1, 0, 2, 1, 0, 0, 0, 3, 1, 1, 2, 1, 0, 2, 3, 1, 1, 1, 3, 0, 0, 2,
-            2, 1, 2, 3, 1, 2, 0, 3, 2, 0, 0, 3, 3, 1, 0, 2, 2, 2, 1, 2, 2, 3, 3, 2, 3, 3, 3, 3, 0,
-            2, 3,
+            4, 4, 4, 4, 0, 1, 3, 0, 1, 0, 1, 1, 0, 2, 1, 0, 0, 0, 3, 1, 1, 2, 1, 0, 2, 3, 1, 1, 1,
+            3, 0, 0, 2, 2, 1, 2, 3, 1, 2, 0, 3, 2, 0, 0, 3, 3, 1, 0, 2, 2, 2, 1, 2, 2, 3, 3, 2, 3,
+            3, 3, 3, 0, 2, 3,
         ),
         (
-            0, 1, 0, 0, 1, 0, 3, 2, 0, 1, 0, 2, 0, 3, 1, 2, 1, 1, 0, 1, 0, 2, 2, 0, 1, 0, 3, 3, 3,
-            1, 2, 2, 0, 3, 0, 2, 0, 2, 1, 3, 2, 1, 3, 1, 2, 3, 2, 3, 1, 1, 1, 2, 2, 2, 3, 3, 0, 3,
-            3, 3,
+            4, 4, 4, 4, 0, 1, 0, 0, 1, 0, 3, 2, 0, 1, 0, 2, 0, 3, 1, 2, 1, 1, 0, 1, 0, 2, 2, 0, 1,
+            0, 3, 3, 3, 1, 2, 2, 0, 3, 0, 2, 0, 2, 1, 3, 2, 1, 3, 1, 2, 3, 2, 3, 1, 1, 1, 2, 2, 2,
+            3, 3, 0, 3, 3, 3,
         ),
     ),
 }
@@ -82,12 +81,12 @@
         size, u = self.length, self.place
 
         def take(slot, into):
-            got = remote(slots.at[slot], slots.at[slot], send.at[0], recv.at[slot], self.spot.at(self.name, 0))
+            got = remote(slots(slot), slots(slot), send.at[0], recv.at[slot], self.spot.at(self.name, 0))
             got.wait_recv()
-            into[...] += slots[slot]
+            into[...] += slots(slot)[...]
 
         def push(k, step, slot):
-            remote(chunk(k), slots.at[slot], send.at[k], recv.at[slot], self.spot.at(self.name, step)).start()
+            remote(chunk(k), slots(slot), send.at[k], recv.at[slot], self.spot.at(self.name, step)).start()
 
         for step in range(size - 1):
             right, left = size - 1 - step, step
@@ -125,7 +124,7 @@
         for k in range(self.length):
             @pl.when(self.place != k)
             def _():
-                remote(chunk(k), slots.at[0], send.at[k], recv.at[0], self.spot.at(self.name, 0)).wait_send()
+                remote(chunk(k), slots(0), send.at[k], recv.at[0], self.spot.at(self.name, 0)).wait_send()
 
     def gather(self, chunk, send, recv):
         size, u = self.length, self.place
@@ -188,11 +187,13 @@
 
 
 def front_kernel(
-    peers, shape, base_ref, probe_ref, patch_ref, amp_ref, grad_ref, light_ref, total_ref,
+    peers, shape, base_ref, probe_ref, patch_ref, amp_ref, dir_ref, pre_ref, sums_ref,
     plus, minus, probe, exits, wave, stacked, own, other, load_sem, send_sem, recv_sem,
-    lit, held, tile_in, tile_all, *rest,
+    lit, held_i, tile_in, tile_all, grad, light_own, prev, sums_in, sums_all, *rest,
 ):
-    slots, sc_s, sc_r, (core_s, core_r, bc_s, bc_r) = rest[0:4], rest[4:8], rest[8:12], rest[12:]
+    islots, isc_s, isc_r, (icore_s, icore_r, ibc_s, ibc_r) = rest[0:4], rest[4:8], rest[8:12], rest[12:16]
+    (core_s, core_r), sc_s, sc_r, ga_s, ga_r = rest[16:18], rest[18:22], rest[22:26], rest[26:30], rest[30:34]
+    back_s, back_r, dir_sem, bc_s, bc_r, out_sem, ready = rest[34:]
     spot = Spot(*shape)
     positions, modes = exits.shape[0], exits.shape[1]
     width = base_ref.shape[1]
@@ -200,6 +201,8 @@
     step = min(64, tile)
     f32, bf16 = jnp.float32, jnp.bfloat16
     y = lax.axis_index("mode")
+    share = Shares(spot, width)
+    pixels = float(width * width)
 
     barrier = pltpu.get_barrier_semaphore()
     for k in range(1, peers):
@@ -213,8 +216,17 @@
 
     for m in range(modes):
         load(m).start()
+    def load_prev(path, m):
+        start = pl.multiple_of(share.base + share.offset[path], 8)
+        return pltpu.make_async_copy(dir_ref.at[:, m, pl.ds(start, share.own), :], prev.at[m], dir_sem.at[m])
+
+    def fetch(path):
+        for m in range(modes):
+            load_prev(path, m).start()
+
+    per_path(spot, shape[2], fetch)
+    sums_in[...] = jnp.zeros_like(sums_in)
     build_tables(base_ref, plus, minus)
-    share = Shares(spot, width)
     pl.semaphore_wait(barrier, peers - 1 + spot.count - 1)
 
     def swap(p, t, k):
@@ -276,9 +288,9 @@
 
     lax.fori_loop(0, positions, forward, 0)
 
-    def give():
+    def give_light():
         away = rows_at(lit, (1 - spot.core) * share.part, share.part)
-        return remote(away, held, core_s.at[0], core_r.at[0], spot.partner())
+        return remote(away, held_i, icore_s.at[0], icore_r.at[0], spot.partner())
 
     def shine(i, carry):
         rows = pl.ds(pl.multiple_of(i * step, step), step)
@@ -289,32 +301,35 @@
         lit[0, rows, :] = acc
         return carry
 
-    def parts(path):
-        sems = [(slots[k], sc_s[k], sc_r[k]) for k in (2 * path, 2 * path + 1)]
-        return share.scatter_parts(path, held, sems)
-
-    def scatter(path):
-        for line, chunk, slot, send, recv in parts(path):
+    def spare(k, slot):
+        return islots[k].at[slot]
+
+    def light_parts(path):
+        sems = [(functools.partial(spare, k), isc_s[k], isc_r[k]) for k in (2 * path, 2 * path + 1)]
+        return share.scatter_parts(path, held_i, sems)
+
+    def light_scatter(path):
+        for line, chunk, slot, send, recv in light_parts(path):
             for _ in line.scatter(chunk, slot, send, recv):
                 pass
-        block = held[0, pl.ds(pl.multiple_of(share.offset[path], 8), share.own), :]
-        light_ref[0] = block
+        block = held_i[0, pl.ds(pl.multiple_of(share.offset[path], 8), share.own), :]
+        light_own[...] = block
         tile_in[...] = fold_lanes(block)
 
-    def scatter_end(path):
-        for line, chunk, slot, send, recv in parts(path):
+    def light_end(path):
+        for line, chunk, slot, send, recv in light_parts(path):
             line.scatter_end(chunk, slot, send, recv)
 
     lax.fori_loop(0, width // step, shine, 0)
-    give().start()
-    give().wait_recv()
-    add_rows(held, lit, share.base, share.part)
-    per_path(spot, shape[2], scatter)
-    for copy in broadcast(spot, tile_in, tile_all, bc_s, bc_r):
+    give_light().start()
+    give_light().wait_recv()
+    add_rows(held_i, lit, share.base, share.part)
+    per_path(spot, shape[2], light_scatter)
+    for copy in broadcast(spot, tile_in, tile_all, ibc_s, ibc_r):
         copy.start()
     tile_all[0] = tile_in[...]
 
-    def backward(p, carry):
+    def unfix(p):
         for t in range(2):
             for k in range(1, peers):
                 swap(p, t, k).wait_recv()
@@ -347,39 +362,157 @@
 
             lax.fori_loop(0, modes, first, 0)
 
-        def second(m, carry):
-            for t in range(2):
-                rows = pl.ds(t * tile, tile)
-                out = jnp.dot(plus[t * width : (t + 1) * width, :], stacked[m], preferred_element_type=f32)
-                for col in range(2):
-                    at = pl.ds(col * tile, tile)
-                    real, imag = out[:tile, col * tile : (col + 1) * tile], out[tile:, col * tile : (col + 1) * tile]
-                    obj_re = patch_ref[p, 0, rows, at].astype(f32)
-                    obj_im = patch_ref[p, 1, rows, at].astype(f32)
-                    diff_re = real - exits[p, m, rows, 2 * col * tile : (2 * col + 1) * tile].astype(f32)
-                    diff_im = imag - exits[p, m, rows, (2 * col + 1) * tile : (2 * col + 2) * tile].astype(f32)
-                    add_re = obj_re * diff_re + obj_im * diff_im
-                    add_im = obj_re * diff_im - obj_im * diff_re
-                    grad_ref[m, 0, rows, at] = jnp.where(p == 0, add_re, grad_ref[m, 0, rows, at] + add_re)
-                    grad_ref[m, 1, rows, at] = jnp.where(p == 0, add_im, grad_ref[m, 1, rows, at] + add_im)
+    def gradient(p, m):
+        for t in range(2):
+            rows = pl.ds(t * tile, tile)
+            out = jnp.dot(plus[t * width : (t + 1) * width, :], stacked[m], preferred_element_type=f32)
+            for col in range(2):
+                at = pl.ds(col * tile, tile)
+                real, imag = out[:tile, col * tile : (col + 1) * tile], out[tile:, col * tile : (col + 1) * tile]
+                obj_re = patch_ref[p, 0, rows, at].astype(f32)
+                obj_im = patch_ref[p, 1, rows, at].astype(f32)
+                diff_re = real - exits[p, m, rows, 2 * col * tile : (2 * col + 1) * tile].astype(f32)
+                diff_im = imag - exits[p, m, rows, (2 * col + 1) * tile : (2 * col + 2) * tile].astype(f32)
+                add_re = obj_re * diff_re + obj_im * diff_im
+                add_im = obj_re * diff_im - obj_im * diff_re
+                grad[m, 0, rows, at] = jnp.where(p == 0, add_re, grad[m, 0, rows, at] + add_re)
+                grad[m, 1, rows, at] = jnp.where(p == 0, add_im, grad[m, 1, rows, at] + add_im)
+
+    def backward(p, carry):
+        unfix(p)
+
+        def one(m, carry):
+            gradient(p, m)
             return carry
 
-        lax.fori_loop(0, modes, second, 0)
+        lax.fori_loop(0, modes, one, 0)
         return carry
 
-    lax.fori_loop(0, positions, backward, 0)
-    for copy in broadcast(spot, tile_in, tile_all, bc_s, bc_r):
+    last = positions - 1
+    lax.fori_loop(0, last, backward, 0)
+    unfix(last)
+    for k in range(1, spot.count):
+        pl.semaphore_signal(ready, inc=1, device_id={"grp": lax.rem(spot.me + k, spot.count)}, device_id_type=MESH)
+    for copy in broadcast(spot, tile_in, tile_all, ibc_s, ibc_r):
         copy.wait()
-    total_ref[...] = jnp.sum(tile_all[...], axis=0)
-    give().wait_send()
-    per_path(spot, shape[2], scatter_end)
+    shift = jnp.sum(tile_all[...]) / pixels
+
+    def held(m):
+        return wave.at[0, m, 0]
+
+    def room(m, k, slot):
+        rows = scatter_sizes(shape, width)[k][1]
+        at = slot * rows + tile
+        if k % 2:
+            return wave.at[1, m, 1, :, pl.ds(pl.multiple_of(slot * rows, 8), rows), :]
+        block = at // tile
+        rem = (lambda a, b: a % b) if isinstance(slot, int) else lax.rem
+        return wave.at[block // 2, m, rem(block, 2), :, pl.ds(pl.multiple_of(rem(at, tile), 8), rows), :]
+
+    def give(m):
+        other = (1 - spot.core) * share.part
+        return remote(
+            rows_at(grad.at[m], other, share.part), held(m), core_s.at[m], core_r.at[m], spot.partner()
+        )
+
+    def scatter_parts(m, path):
+        sems = [(functools.partial(room, m, k), sc_s[k].at[m], sc_r[k].at[m]) for k in (2 * path, 2 * path + 1)]
+        return share.scatter_parts(path, held(m), sems)
+
+    def gather_parts(m, path):
+        sems = [(ga_s[k].at[m], ga_r[k].at[m]) for k in (2 * path, 2 * path + 1)]
+        return share.gather_parts(path, probe.at[m], sems)
+
+    def home(m):
+        block = rows_at(probe.at[m], share.base, share.part)
+        return remote(block, block, back_s.at[m], back_r.at[m], spot.partner())
+
+    def stream(m, path):
+        give(m).wait_recv()
+        add_rows(held(m), grad.at[m], share.base, share.part)
+        for line, chunk, slot, send, recv in scatter_parts(m, path):
+            yield from line.scatter(chunk, slot, send, recv)
+        rows = pl.ds(pl.multiple_of(share.offset[path], 8), share.own)
+        to = pl.ds(pl.multiple_of(share.base + share.offset[path], 8), share.own)
+        light = light_own[...]
+        load_prev(path, m).wait()
+        g_re, g_im = held(m)[0, rows, :], held(m)[1, rows, :]
+        d_re, d_im = prev[m, 0], prev[m, 1]
+        den = light + shift
+        p_re, p_im = g_re / den, g_im / den
+        probe[m, 0, to, :] = p_re
+        probe[m, 1, to, :] = p_im
+        (line, chunk, send, recv), later = gather_parts(m, path)
+        walk = line.gather(chunk, send, recv)
+        next(walk, None)
+        terms = (
+            g_re * p_re + g_im * p_im,
+            g_re * d_re + g_im * d_im,
+            light * (p_re * p_re + p_im * p_im),
+            light * (p_re * d_re + p_im * d_im),
+            light * (d_re * d_re + d_im * d_im),
+        )
+        for k, term in enumerate(terms):
+            row = 5 * m + k
+            sums_in[row : row + 1, :] = jnp.sum(fold_lanes(term), axis=0, keepdims=True)
+        yield
+        yield from walk
+        line, chunk, send, recv = later
+        yield from line.gather(chunk, send, recv)
+        home(m).start()
+
+    streams = [[stream(m, path) for m in range(modes)] for path in range(2)]
+    orders = [list(turns(shape, modes, path)) for path in range(2)]
+
+    def advance(path):
+        order = orders[path]
+        while order and order[0] != modes:
+            next(streams[path][order.pop(0)], None)
+
+    for m in range(modes):
+        gradient(last, m)
+        if m == 0:
+            pl.semaphore_wait(ready, spot.count - 1)
+        give(m).start()
+        for path in range(2):
+            orders[path].pop(0)
+        per_path(spot, shape[2], advance)
+    for copy in broadcast(spot, sums_in, sums_all, bc_s, bc_r):
+        copy.start()
+    sums_all[0] = sums_in[...]
+
+    def out(m):
+        return pltpu.make_async_copy(probe.at[m], pre_ref.at[m], out_sem.at[m])
+
+    for m in range(modes):
+        home(m).wait_recv()
+        out(m).start()
+    for copy in broadcast(spot, sums_in, sums_all, bc_s, bc_r):
+        copy.wait()
+    sums_ref[...] = jnp.sum(sums_all[...], axis=0)
+
+    def close(path):
+        light_end(path)
+        for m in range(modes):
+            for line, chunk, slot, send, recv in scatter_parts(m, path):
+                line.scatter_end(chunk, slot, send, recv)
+            for line, chunk, send, recv in gather_parts(m, path):
+                line.gather_end(chunk, send, recv)
+
+    give_light().wait_send()
+    for m in range(modes):
+        give(m).wait_send()
+        home(m).wait_send()
+    per_path(spot, shape[2], close)
+    for m in range(modes):
+        out(m).wait()
     for p in range(positions):
         for t in range(2):
             for k in range(1, peers):
                 swap(p, t, k).wait_send()
 
 
-def front(base, probe, patches, amplitude):
+def front(base, probe, patches, amplitude, direction):
     modes, width = probe.shape[1], probe.shape[2]
     positions = patches.shape[0]
     peers = lax.axis_size("mode")
@@ -388,17 +521,22 @@
     f32, bf16 = jnp.float32, jnp.bfloat16
     vmem = pl.BlockSpec(memory_space=pltpu.VMEM)
     shape = split_lines(lax.axis_size("grp"))
+    outer, inner, cores = shape
+    assert cores == 2 and positions >= 2
     sizes = scatter_sizes(shape, width)
     count, lanes = lax.axis_size("grp"), min(128, width)
+    own = sizes[1][1]
+    back_sizes = [outer, inner, inner, outer]
+    sum_rows = -(-5 * modes // 8) * 8
+    hbm = pl.BlockSpec(memory_space=pl.ANY)
     flops = positions * modes * 2 * 16 * width**3
     return pl.pallas_call(
         functools.partial(front_kernel, peers, shape),
-        in_specs=[vmem, pl.BlockSpec(memory_space=pl.ANY), vmem, vmem],
-        out_specs=[vmem, vmem, vmem],
+        in_specs=[vmem, hbm, vmem, vmem, hbm],
+        out_specs=[hbm, vmem],
         out_shape=[
             jax.ShapeDtypeStruct((modes, 2, width, width), f32),
-            jax.ShapeDtypeStruct((1, sizes[1][1], width), f32),
-            jax.ShapeDtypeStruct((8, lanes), f32),
+            jax.ShapeDtypeStruct((sum_rows, lanes), f32),
         ],
         scratch_shapes=[
             pltpu.VMEM((2 * width, 2 * width), bf16),
@@ -416,6 +554,11 @@
             pltpu.VMEM((1, width // shape[2], width), f32),
             pltpu.VMEM((8, lanes), f32),
             pltpu.VMEM((count, 8, lanes), f32),
+            pltpu.VMEM((modes, 2, width, width), f32),
+            pltpu.VMEM((own, width), f32),
+            pltpu.VMEM((modes, 2, own, width), f32),
+            pltpu.VMEM((sum_rows, lanes), f32),
+            pltpu.VMEM((count, sum_rows, lanes), f32),
             *[pltpu.VMEM((n + 1, 1, rows, width), f32) for n, rows in sizes],
             *[dma((n,)) for n, _ in sizes],
             *[dma((n + 1,)) for n, _ in sizes],
@@ -423,11 +566,24 @@
             dma((1,)),
             dma((count,)),
             dma((count,)),
+            dma((modes,)),
+            dma((modes,)),
+            *[dma((modes, n)) for n, _ in sizes],
+            *[dma((modes, n + 1)) for n, _ in sizes],
+            *[dma((modes, 2, n)) for n in back_sizes],
+            *[dma((modes, n)) for n in back_sizes],
+            dma((modes,)),
+            dma((modes,)),
+            dma((modes,)),
+            dma((count,)),
+            dma((count,)),
+            dma((modes,)),
+            pltpu.SemaphoreType.REGULAR,
         ],
         compiler_params=pltpu.CompilerParams(collective_id=1, has_side_effects=True, vmem_limit_bytes=FRONT_LIMIT),
         cost_estimate=pl.CostEstimate(flops=flops, bytes_accessed=0, transcendentals=0),
         name="front",
-    )(base, probe, patches, amplitude)
+    )(base, probe, patches, amplitude, direction)
 
 
 def split_lines(count):
@@ -500,174 +656,13 @@
             act(path)
 
 
-def reduce_kernel(
-    shape, modes, width, grad_ref, light_ref, total_ref, dir_ref, pre_ref, sums_ref,
-    held, prev, sums_in, sums_all, *rest,
-):
-    outer, inner, cores = shape
-    spot = Spot(outer, inner, cores)
-    share = Shares(spot, width)
-    slots, (core_s, core_r), sc_s, sc_r, ga_s, ga_r, (back_s, back_r, dir_sem, bc_s, bc_r) = (
-        rest[0:4], rest[4:6], rest[6:10], rest[10:14], rest[14:18], rest[18:22], rest[22:]
-    )
-    pixels = float(width * width)
-
-    barrier = pltpu.get_barrier_semaphore()
-    for step in range(1, spot.count):
-        to = lax.rem(spot.me + step, spot.count)
-        pl.semaphore_signal(barrier, inc=1, device_id={"grp": to}, device_id_type=MESH)
-
-    def load(path, m):
-        start = pl.multiple_of(share.base + share.offset[path], 8)
-        return pltpu.make_async_copy(dir_ref.at[:, m, pl.ds(start, share.own), :], prev.at[m], dir_sem.at[m])
-
-    def fetch(path):
-        for m in range(modes):
-            load(path, m).start()
-
-    per_path(spot, cores, fetch)
-    sums_in[...] = jnp.zeros_like(sums_in)
-    pl.semaphore_wait(barrier, spot.count - 1)
-
-    def give(m):
-        other = (1 - spot.core) * share.part
-        return remote(
-            rows_at(grad_ref.at[m], other, share.part), held.at[m], core_s.at[m], core_r.at[m], spot.partner()
-        )
-
-    for m in range(modes):
-        give(m).start()
-    shift = jnp.sum(total_ref[...]) / pixels
-
-    def scatter_parts(m, path):
-        sems = [(slots[k].at[m], sc_s[k].at[m], sc_r[k].at[m]) for k in (2 * path, 2 * path + 1)]
-        return share.scatter_parts(path, held.at[m], sems)
-
-    def gather_parts(m, path):
-        sems = [(ga_s[k].at[m], ga_r[k].at[m]) for k in (2 * path, 2 * path + 1)]
-        return share.gather_parts(path, pre_ref.at[m], sems)
-
-    def home(m):
-        block = rows_at(pre_ref.at[m], share.base, share.part)
-        return remote(block, block, back_s.at[m], back_r.at[m], spot.partner())
-
-    def stream(m, path):
-        give(m).wait_recv()
-        add_rows(held.at[m], grad_ref.at[m], share.base, share.part)
-        for line, chunk, slot, send, recv in scatter_parts(m, path):
-            yield from line.scatter(chunk, slot, send, recv)
-        rows = pl.ds(pl.multiple_of(share.offset[path], 8), share.own)
-        to = pl.ds(pl.multiple_of(share.base + share.offset[path], 8), share.own)
-        light = light_ref[0]
-        load(path, m).wait()
-        g_re, g_im = held[m, 0, rows, :], held[m, 1, rows, :]
-        d_re, d_im = prev[m, 0], prev[m, 1]
-        den = light + shift
-        p_re, p_im = g_re / den, g_im / den
-        pre_ref[m, 0, to, :] = p_re
-        pre_ref[m, 1, to, :] = p_im
-        (line, chunk, send, recv), later = gather_parts(m, path)
-        walk = line.gather(chunk, send, recv)
-        next(walk, None)
-        terms = (
-            g_re * p_re + g_im * p_im,
-            g_re * d_re + g_im * d_im,
-            light * (p_re * p_re + p_im * p_im),
-            light * (p_re * d_re + p_im * d_im),
-            light * (d_re * d_re + d_im * d_im),
-        )
-        for k, term in enumerate(terms):
-            row = 5 * m + k
-            sums_in[row : row + 1, :] = jnp.sum(fold_lanes(term), axis=0, keepdims=True)
-        if m == modes - 1:
-            told.append(True)
-        yield
-        yield from walk
-        line, chunk, send, recv = later
-        yield from line.gather(chunk, send, recv)
-        home(m).start()
-
-    told = []
-
-    def share_sums():
-        for copy in broadcast(spot, sums_in, sums_all, bc_s, bc_r):
-            copy.start()
-
-    def run(path):
-        told.clear()
-        streams = [stream(m, path) for m in range(modes)]
-        done = set()
-        for m in turns(shape, modes, path):
-            if m in done:
-                continue
-            if next(streams[m], done) is done:
-                done.add(m)
-        share_sums()
-        sums_all[0] = sums_in[...]
-        for copy in broadcast(spot, sums_in, sums_all, bc_s, bc_r):
-            copy.wait_recv()
-        for m in range(modes):
-            home(m).wait_recv()
-        for m in range(modes):
-            give(m).wait_send()
-            for line, chunk, slot, send, recv in scatter_parts(m, path):
-                line.scatter_end(chunk, slot, send, recv)
-            for line, chunk, send, recv in gather_parts(m, path):
-                line.gather_end(chunk, send, recv)
-            home(m).wait_send()
-        for copy in broadcast(spot, sums_in, sums_all, bc_s, bc_r):
-            copy.wait_send()
-
-    per_path(spot, cores, run)
-    sums_ref[...] = jnp.sum(sums_all[...], axis=0)
-
-
 def turns(shape, modes, path):
     key = (*shape, modes)
     if key in ORDERS:
         return ORDERS[key][path]
     steps = 8 * (shape[0] + shape[1])
     events = sorted((k + (3 * m) // 2, m) for m in range(modes) for k in range(steps))
-    return [m for _, m in events]
-
-
-def reduce_grads(part, light, total, direction):
-    modes, _, width, _ = part.shape
-    shape = split_lines(lax.axis_size("grp"))
-    outer, inner, cores = shape
-    count = outer * inner * cores
-    sizes = scatter_sizes(shape, width)
-    own = sizes[1][1]
-    back_sizes = [outer, inner, inner, outer]
-    sum_rows = -(-5 * modes // 8) * 8
-    lanes = min(128, width)
-    dma = pltpu.SemaphoreType.DMA
-    f32 = jnp.float32
-    scratch = [
-        pltpu.VMEM((modes, 2, width // cores, width), f32),
-        pltpu.VMEM((modes, 2, own, width), f32),
-        pltpu.VMEM((sum_rows, lanes), f32),
-        pltpu.VMEM((count, sum_rows, lanes), f32),
-    ]
-    scratch += [pltpu.VMEM((modes, n + 1, 2, rows, width), f32) for n, rows in sizes]
-    scratch += [dma((modes,)), dma((modes,))]
-    scratch += [dma((modes, n)) for n, _ in sizes] + [dma((modes, n + 1)) for n, _ in sizes]
-    scratch += [dma((modes, 2, n)) for n in back_sizes] + [dma((modes, n)) for n in back_sizes]
-    scratch += [dma((modes,)), dma((modes,)), dma((modes,)), dma((count,)), dma((count,))]
-    vmem = pl.BlockSpec(memory_space=pltpu.VMEM)
-    return pl.pallas_call(
-        functools.partial(reduce_kernel, shape, modes, width),
-        in_specs=[vmem, vmem, vmem, pl.BlockSpec(memory_space=pl.ANY)],
-        out_specs=[vmem, vmem],
-        out_shape=[
-            jax.ShapeDtypeStruct(part.shape, f32),
-            jax.ShapeDtypeStruct((sum_rows, lanes), f32),
-        ],
-        scratch_shapes=scratch,
-        compiler_params=pltpu.CompilerParams(collective_id=0, has_side_effects=True, vmem_limit_bytes=REDUCE_LIMIT),
-        cost_estimate=pl.CostEstimate(flops=10**10, bytes_accessed=0, transcendentals=0),
-        name="reduce",
-    )(part, light, total, direction)
+    return [modes] * modes + [m for _, m in events]
 
 
 def finish_kernel(norm_ref, sums_ref, pre_ref, probe_ref, dir_ref, new_probe, new_dir, new_norm, kept):
@@ -785,8 +780,7 @@
 def on_device(probe, prev_direction, prev_norm, object_tile, offsets, amplitude):
     width = probe.shape[2]
     patches = cut(offsets, object_tile, width)
-    part, light, total = front(base_table(width), probe, patches, amplitude)
-    pre, sums = reduce_grads(part, light, total, prev_direction)
+    pre, sums = front(base_table(width), probe, patches, amplitude, prev_direction)
     return tuple(finish(prev_norm, sums, pre, probe, prev_direction))
 
 

time: 234 us -> 218 us (0.932)
  local copies, waits for them, and re-layouts: 18.5 us -> 3.42 us
    pallas_call x1 -> x0, Pallas kernels: 117 us -> none  [reduce_grads(): pl.pallas_call(functools.partial(reduce_kernel, shape, modes, width), in_...]
    pallas_call x1, Pallas kernels: 85.7 us -> 194 us  [front(): pl.pallas_call(functools.partial(front_kernel, peers, shape), in_specs=[v...]
    unnamed x22 -> x6, local copies, waits for them, and re-layouts: 18.5 us -> 3.42 us
    pallas_call x1, Pallas kernels: 8.79 us -> 16 us  [finish(): pl.pallas_call(finish_kernel, grid=(modes, width // rows), in_specs=[smem...]
where the time goes in v5:
time: 218 us
  Pallas kernels  214 us (98%)
  local copies, waits for them, and re-layouts  3.42 us (2%)
    pallas_call x1, Pallas kernels, front(): pl.pallas_call(functools.partial(front_kernel, peers, shape), in_specs=[v...  194 us
    pallas_call x1, Pallas kernels, finish(): pl.pallas_call(finish_kernel, grid=(modes, width // rows), in_specs=[smem...  16 us

profile of v5, /device:TPU:0, one launch (start us, length us, event | category | flops | bytes accessed | tf_op | source)
XLA Modules:
  0.0 218.1 jit_solution(1234889492513376980)
XLA Ops:
  0.6 0.0 copy-start.1
  0.6 1.4 copy-done.1
  2.1 0.0 copy-start.2
  2.1 0.7 copy-done.2
  2.7 3.5 %cut.1.patch_ref = bf16[2,2,512,512]{3,2,1,0:T(8,128)(2,1)S(1)} custom-call(s32[2,2]{1,0:T(2,128)S(1)} %copy-done.2, bf16[2,640,640]{2,1,0:T(8,128)(2,1)S(1)} %copy-done.1), custom_call_target="tpu_custom_call" | custom-call | tf_op jit(solution)/shard_map/cut/pallas_call | solution.py:765
  6.3 0.0 copy-start
  6.3 1.3 copy-done
  7.6 194.4 %front.1 = (f32[4,2,512,512]{3,2,1,0:T(8,128)}, f32[24,128]{1,0:T(8,128)}) custom-call(bf16[2,512,512]{2,1,0:T(8,128)(2,1)} %constant.2.clone.base_ref, f32[2,4,512,512]{3,2,1,0:T(8,128)} %probe_ref.3, bf16[2,2,512,512]{3,2,1,0:T(8,128)(2,1)} %copy-done, bf16[2,512,512]{2,1,0:T(8,128)(2,1)} %amp_ref.1, f32[2,4,512,512]{3,2,1,0:T(8,128)} %dir_ref.3), custom_call_target="tpu_custom_call" | custom-call | flops 34359738368 | tf_op jit(solution)/shard_map/front/pallas_call | solution.py:533
  202.1 16.0 %finish.1 = (f32[2,4,512,512]{3,2,1,0:T(8,128)}, f32[2,4,512,512]{3,2,1,0:T(8,128)}, f32[4]{0:T(128)}) custom-call(f32[4]{0:T(128)} %norm_ref.1, f32[24,128]{1,0:T(8,128)} %get-tuple-element.5.sums_ref, f32[4,2,512,512]{3,2,1,0:T(8,128)} %get-tuple-element.6.pre_ref, f32[2,4,512,512]{3,2,1,0:T(8,128)} %probe_ref.3, f32[2,4,512,512]{3,2,1,0:T(8,128)} %dir_ref.3), custom_call_target="tpu_custom_call" | custom-call | tf_op jit(solution)/shard_map/finish/pallas_call | solution.py:707
Async XLA Ops:
  0.6 1.4 copy-start.1
  2.1 0.7 copy-start.2
  6.3 1.3 copy-start

commit v6 on v5

--- a/solution.py
+++ b/solution.py
@@ -17,14 +17,14 @@
 ORDERS = {
     (4, 2, 2, 4): (
         (
-            4, 4, 4, 4, 0, 1, 3, 0, 1, 0, 1, 1, 0, 2, 1, 0, 0, 0, 3, 1, 1, 2, 1, 0, 2, 3, 1, 1, 1,
-            3, 0, 0, 2, 2, 1, 2, 3, 1, 2, 0, 3, 2, 0, 0, 3, 3, 1, 0, 2, 2, 2, 1, 2, 2, 3, 3, 2, 3,
-            3, 3, 3, 0, 2, 3,
+            4, 4, 0, 4, 1, 4, 2, 0, 1, 1, 0, 3, 0, 1, 1, 1, 0, 0, 1, 2, 1, 0, 3, 0, 3, 2, 1, 3, 3,
+            3, 0, 2, 1, 1, 2, 2, 0, 0, 1, 2, 3, 3, 2, 0, 3, 0, 2, 2, 3, 1, 1, 0, 2, 3, 2, 2, 3, 3,
+            1, 3, 0, 2, 3, 2,
         ),
         (
-            4, 4, 4, 4, 0, 1, 0, 0, 1, 0, 3, 2, 0, 1, 0, 2, 0, 3, 1, 2, 1, 1, 0, 1, 0, 2, 2, 0, 1,
-            0, 3, 3, 3, 1, 2, 2, 0, 3, 0, 2, 0, 2, 1, 3, 2, 1, 3, 1, 2, 3, 2, 3, 1, 1, 1, 2, 2, 2,
-            3, 3, 0, 3, 3, 3,
+            4, 4, 0, 4, 1, 0, 0, 4, 1, 0, 2, 3, 0, 0, 2, 0, 1, 3, 0, 2, 1, 0, 1, 1, 0, 2, 2, 0, 2,
+            1, 0, 1, 2, 3, 3, 1, 3, 2, 0, 2, 3, 1, 3, 3, 2, 1, 2, 1, 3, 0, 3, 2, 1, 0, 2, 3, 2, 1,
+            3, 1, 2, 3, 3, 3,
         ),
     ),
 }
@@ -81,12 +81,12 @@
         size, u = self.length, self.place
 
         def take(slot, into):
-            got = remote(slots(slot), slots(slot), send.at[0], recv.at[slot], self.spot.at(self.name, 0))
+            got = remote(slots(slot), slots(slot), send().at[0], recv().at[slot], self.spot.at(self.name, 0))
             got.wait_recv()
             into[...] += slots(slot)[...]
 
         def push(k, step, slot):
-            remote(chunk(k), slots(slot), send.at[k], recv.at[slot], self.spot.at(self.name, step)).start()
+            remote(chunk(k), slots(slot), send().at[k], recv().at[slot], self.spot.at(self.name, step)).start()
 
         for step in range(size - 1):
             right, left = size - 1 - step, step
@@ -124,19 +124,19 @@
         for k in range(self.length):
             @pl.when(self.place != k)
             def _():
-                remote(chunk(k), slots(0), send.at[k], recv.at[0], self.spot.at(self.name, 0)).wait_send()
+                remote(chunk(k), slots(0), send().at[k], recv().at[0], self.spot.at(self.name, 0)).wait_send()
 
     def gather(self, chunk, send, recv):
         size, u = self.length, self.place
 
         def push(k, way, step):
-            remote(chunk(k), chunk(k), send.at[way, k], recv.at[k], self.spot.at(self.name, step)).start()
+            remote(chunk(k), chunk(k), send().at[way, k], recv().at[k], self.spot.at(self.name, step)).start()
 
         def take(k):
-            remote(chunk(k), chunk(k), send.at[0, 0], recv.at[k], self.spot.at(self.name, 0)).wait_recv()
+            remote(chunk(k), chunk(k), send().at[0, 0], recv().at[k], self.spot.at(self.name, 0)).wait_recv()
 
         for step in range(size):
-            low, high = u - step, u + step
+            low = u - step
 
             @pl.when(low >= 0)
             def _():
@@ -149,6 +149,7 @@
 
             if size > 2 and step > 0:
                 yield
+            high = u + step
 
             @pl.when(high < size)
             def _():
@@ -168,7 +169,7 @@
             for way in range(2):
                 @pl.when((u < size - 1) & (u >= k) if way == 0 else (u > 0) & (u <= k))
                 def _():
-                    remote(chunk(k), chunk(k), send.at[way, k], recv.at[k], self.spot.at(self.name, 0)).wait_send()
+                    remote(chunk(k), chunk(k), send().at[way, k], recv().at[k], self.spot.at(self.name, 0)).wait_send()
 
 
 def build_tables(base_ref, plus, minus):
@@ -186,14 +187,18 @@
                 ref[r + tile : r + width, c : c + tile] = lower
 
 
+def pick(ref, *index):
+    return (lambda: ref.at[index]) if index else (lambda: ref)
+
+
 def front_kernel(
-    peers, shape, base_ref, probe_ref, patch_ref, amp_ref, dir_ref, pre_ref, sums_ref,
+    peers, shape, base_ref, probe_ref, patch_ref, amp_hbm, dir_ref, pre_ref, sums_ref,
     plus, minus, probe, exits, wave, stacked, own, other, load_sem, send_sem, recv_sem,
     lit, held_i, tile_in, tile_all, grad, light_own, prev, sums_in, sums_all, *rest,
 ):
     islots, isc_s, isc_r, (icore_s, icore_r, ibc_s, ibc_r) = rest[0:4], rest[4:8], rest[8:12], rest[12:16]
     (core_s, core_r), sc_s, sc_r, ga_s, ga_r = rest[16:18], rest[18:22], rest[22:26], rest[26:30], rest[30:34]
-    back_s, back_r, dir_sem, bc_s, bc_r, out_sem, ready = rest[34:]
+    back_s, back_r, dir_sem, bc_s, bc_r, out_sem, ready, amp_ref, amp_sem = rest[34:]
     spot = Spot(*shape)
     positions, modes = exits.shape[0], exits.shape[1]
     width = base_ref.shape[1]
@@ -216,6 +221,8 @@
 
     for m in range(modes):
         load(m).start()
+    amp_load = pltpu.make_async_copy(amp_hbm, amp_ref, amp_sem.at[0])
+    amp_load.start()
     def load_prev(path, m):
         start = pl.multiple_of(share.base + share.offset[path], 8)
         return pltpu.make_async_copy(dir_ref.at[:, m, pl.ds(start, share.own), :], prev.at[m], dir_sem.at[m])
@@ -227,7 +234,6 @@
     per_path(spot, shape[2], fetch)
     sums_in[...] = jnp.zeros_like(sums_in)
     build_tables(base_ref, plus, minus)
-    pl.semaphore_wait(barrier, peers - 1 + spot.count - 1)
 
     def swap(p, t, k):
         rows = pl.ds(t * tile, tile)
@@ -282,6 +288,11 @@
                 return carry
 
             lax.fori_loop(0, modes, second, 0)
+            if t == 0:
+                @pl.when(p == 0)
+                def _():
+                    pl.semaphore_wait(barrier, peers - 1 + spot.count - 1)
+
             for k in range(1, peers):
                 swap(p, t, k).start()
         return carry
@@ -305,8 +316,8 @@
         return islots[k].at[slot]
 
     def light_parts(path):
-        sems = [(functools.partial(spare, k), isc_s[k], isc_r[k]) for k in (2 * path, 2 * path + 1)]
-        return share.scatter_parts(path, held_i, sems)
+        sems = [(functools.partial(spare, k), pick(isc_s[k]), pick(isc_r[k])) for k in (2 * path, 2 * path + 1)]
+        return share.scatter_parts(path, pick(held_i), sems)
 
     def light_scatter(path):
         for line, chunk, slot, send, recv in light_parts(path):
@@ -389,6 +400,7 @@
         return carry
 
     last = positions - 1
+    amp_load.wait()
     lax.fori_loop(0, last, backward, 0)
     unfix(last)
     for k in range(1, spot.count):
@@ -416,16 +428,24 @@
         )
 
     def scatter_parts(m, path):
-        sems = [(functools.partial(room, m, k), sc_s[k].at[m], sc_r[k].at[m]) for k in (2 * path, 2 * path + 1)]
-        return share.scatter_parts(path, held(m), sems)
+        sems = [(functools.partial(room, m, k), pick(sc_s[k], m), pick(sc_r[k], m)) for k in (2 * path, 2 * path + 1)]
+        return share.scatter_parts(path, functools.partial(held, m), sems)
 
     def gather_parts(m, path):
-        sems = [(ga_s[k].at[m], ga_r[k].at[m]) for k in (2 * path, 2 * path + 1)]
-        return share.gather_parts(path, probe.at[m], sems)
+        sems = [(pick(ga_s[k], m), pick(ga_r[k], m)) for k in (2 * path, 2 * path + 1)]
+        return share.gather_parts(path, pick(probe, m), sems)
 
     def home(m):
         block = rows_at(probe.at[m], share.base, share.part)
         return remote(block, block, back_s.at[m], back_r.at[m], spot.partner())
+
+    def out(m, core, k):
+        part = core * share.part
+        return pltpu.make_async_copy(
+            rows_at(probe.at[m], part, share.part), rows_at(pre_ref.at[m], part, share.part), out_sem.at[m, k]
+        )
+
+    told = [0, 0]
 
     def stream(m, path):
         give(m).wait_recv()
@@ -455,11 +475,16 @@
         for k, term in enumerate(terms):
             row = 5 * m + k
             sums_in[row : row + 1, :] = jnp.sum(fold_lanes(term), axis=0, keepdims=True)
+        told[path] += 1
+        if told[path] == modes:
+            for copy in broadcast(spot, sums_in, sums_all, bc_s, bc_r):
+                copy.start()
         yield
         yield from walk
         line, chunk, send, recv = later
         yield from line.gather(chunk, send, recv)
         home(m).start()
+        out(m, spot.core, 0).start()
 
     streams = [[stream(m, path) for m in range(modes)] for path in range(2)]
     orders = [list(turns(shape, modes, path)) for path in range(2)]
@@ -477,16 +502,11 @@
         for path in range(2):
             orders[path].pop(0)
         per_path(spot, shape[2], advance)
-    for copy in broadcast(spot, sums_in, sums_all, bc_s, bc_r):
-        copy.start()
     sums_all[0] = sums_in[...]
-
-    def out(m):
-        return pltpu.make_async_copy(probe.at[m], pre_ref.at[m], out_sem.at[m])
 
     for m in range(modes):
         home(m).wait_recv()
-        out(m).start()
+        out(m, 1 - spot.core, 1).start()
     for copy in broadcast(spot, sums_in, sums_all, bc_s, bc_r):
         copy.wait()
     sums_ref[...] = jnp.sum(sums_all[...], axis=0)
@@ -505,7 +525,8 @@
         home(m).wait_send()
     per_path(spot, shape[2], close)
     for m in range(modes):
-        out(m).wait()
+        out(m, spot.core, 0).wait()
+        out(m, 1 - spot.core, 1).wait()
     for p in range(positions):
         for t in range(2):
             for k in range(1, peers):
@@ -532,7 +553,7 @@
     flops = positions * modes * 2 * 16 * width**3
     return pl.pallas_call(
         functools.partial(front_kernel, peers, shape),
-        in_specs=[vmem, hbm, vmem, vmem, hbm],
+        in_specs=[vmem, hbm, vmem, hbm, hbm],
         out_specs=[hbm, vmem],
         out_shape=[
             jax.ShapeDtypeStruct((modes, 2, width, width), f32),
@@ -577,8 +598,10 @@
             dma((modes,)),
             dma((count,)),
             dma((count,)),
-            dma((modes,)),
+            dma((modes, 2)),
             pltpu.SemaphoreType.REGULAR,
+            pltpu.VMEM(amplitude.shape, amplitude.dtype),
+            dma((1,)),
         ],
         compiler_params=pltpu.CompilerParams(collective_id=1, has_side_effects=True, vmem_limit_bytes=FRONT_LIMIT),
         cost_estimate=pl.CostEstimate(flops=flops, bytes_accessed=0, transcendentals=0),
@@ -609,13 +632,13 @@
         self.offset = (self.group[0] + spot.outer * self.own, self.group[1] + spot.inner * self.own)
 
     def scatter_parts(self, path, held, sems):
-        top = lambda k: rows_at(held, k * self.big[path], self.big[path])
-        low = lambda k: rows_at(held, self.group[path] + k * self.own, self.own)
+        top = lambda k: rows_at(held(), k * self.big[path], self.big[path])
+        low = lambda k: rows_at(held(), self.group[path] + k * self.own, self.own)
         return [(line, chunk) + pair for line, chunk, pair in zip(self.lines[path], (top, low), sems)]
 
     def gather_parts(self, path, whole_ref, sems):
-        low = lambda k: rows_at(whole_ref, self.base + self.group[path] + k * self.own, self.own)
-        top = lambda k: rows_at(whole_ref, self.base + k * self.big[path], self.big[path])
+        low = lambda k: rows_at(whole_ref(), self.base + self.group[path] + k * self.own, self.own)
+        top = lambda k: rows_at(whole_ref(), self.base + k * self.big[path], self.big[path])
         return [(line, chunk) + pair for line, chunk, pair in zip(self.lines[path][::-1], (low, top), sems)]
 
 
@@ -701,7 +724,7 @@
 
 def finish(prev_norm, sums, pre, probe, direction):
     modes, width = probe.shape[1], probe.shape[2]
-    rows = min(256, width)
+    rows = min(512, width)
     block = pl.BlockSpec((2, 1, rows, width), lambda m, r: (0, m, r, 0))
     smem = pl.BlockSpec(memory_space=pltpu.SMEM)
     return pl.pallas_call(
@@ -769,6 +792,7 @@
         out_shape=jax.ShapeDtypeStruct((positions, 2, width, width), jnp.bfloat16),
         scratch_shapes=[pltpu.VMEM((2, tile.shape[1] + 8, tile.shape[2]), jnp.float32)],
         compiler_params=pltpu.CompilerParams(vmem_limit_bytes=CUT_LIMIT),
+        cost_estimate=pl.CostEstimate(flops=10**9, bytes_accessed=0, transcendentals=0),
         name="cut",
     )(offsets, tile)
 

time: 218 us -> 209 us (0.959)
  Pallas kernels: 214 us -> 205 us
    pallas_call x1, Pallas kernels: 194 us -> 187 us  [front(): pl.pallas_call(functools.partial(front_kernel, peers, shape), in_specs=[v...]
where the time goes in v6:
time: 209 us
  Pallas kernels  205 us (98%)
  local copies, waits for them, and re-layouts  3.42 us (2%)
    pallas_call x1, Pallas kernels, front(): pl.pallas_call(functools.partial(front_kernel, peers, shape), in_specs=[v...  187 us
    pallas_call x1, Pallas kernels, finish(): pl.pallas_call(finish_kernel, grid=(modes, width // rows), in_specs=[smem...  14.1 us

profile of v6, /device:TPU:0, one launch (start us, length us, event | category | flops | bytes accessed | tf_op | source)
XLA Modules:
  0.0 209.0 jit_solution(9252548006917880008)
XLA Ops:
  0.6 0.0 copy-start.1
  0.6 1.4 copy-done.1
  2.1 0.0 copy-start.2
  2.1 0.7 copy-done.2
  2.7 3.5 %cut.1.patch_ref = bf16[2,2,512,512]{3,2,1,0:T(8,128)(2,1)S(1)} custom-call(s32[2,2]{1,0:T(2,128)S(1)} %copy-done.2, bf16[2,640,640]{2,1,0:T(8,128)(2,1)S(1)} %copy-done.1), custom_call_target="tpu_custom_call" | custom-call | flops 1000000000 | tf_op jit(solution)/shard_map/cut/pallas_call | solution.py:788
  6.3 0.0 copy-start
  6.3 1.3 copy-done
  7.6 187.3 %front.1 = (f32[4,2,512,512]{3,2,1,0:T(8,128)}, f32[24,128]{1,0:T(8,128)}) custom-call(bf16[2,512,512]{2,1,0:T(8,128)(2,1)} %constant.2.clone.base_ref, f32[2,4,512,512]{3,2,1,0:T(8,128)} %probe_ref.3, bf16[2,2,512,512]{3,2,1,0:T(8,128)(2,1)} %copy-done, bf16[2,512,512]{2,1,0:T(8,128)(2,1)} %amp_hbm.1, f32[2,4,512,512]{3,2,1,0:T(8,128)} %dir_ref.3), custom_call_target="tpu_custom_call" | custom-call | flops 34359738368 | tf_op jit(solution)/shard_map/front/pallas_call | solution.py:554
  195.0 14.1 %finish.1 = (f32[2,4,512,512]{3,2,1,0:T(8,128)}, f32[2,4,512,512]{3,2,1,0:T(8,128)}, f32[4]{0:T(128)}) custom-call(f32[4]{0:T(128)} %norm_ref.1, f32[24,128]{1,0:T(8,128)} %get-tuple-element.5.sums_ref, f32[4,2,512,512]{3,2,1,0:T(8,128)} %get-tuple-element.6.pre_ref, f32[2,4,512,512]{3,2,1,0:T(8,128)} %probe_ref.3, f32[2,4,512,512]{3,2,1,0:T(8,128)} %dir_ref.3), custom_call_target="tpu_custom_call" | custom-call | tf_op jit(solution)/shard_map/finish/pallas_call | solution.py:730
Async XLA Ops:
  0.6 1.4 copy-start.1
  2.1 0.7 copy-start.2
  6.3 1.3 copy-start
